TPU v7x, 32 devices: a whole 2x2x4 slice. The times are simulated.
32 devices in a mesh: scene: 2 (over y), pulse: 8 (over z, x), scat: 2 (over core).
Axes of the slice: x: 2, y: 2, z: 4, core: 2. Of those that a mesh axis runs over, the one named last changes fastest.
Arguments:
- positions: float32 [32768], P(('scene', 'scat')), parts along dimension 0, may hold values from -1000 to 1000
- amplitude: float32 [2, 32768], P(None, ('scene', 'scat')), parts along dimension 1, may hold values from -3 to 3
- range_cells: int32 [32768], P(('scene', 'scat')), parts along dimension 0, may hold values from 0 to 1007
- bounce: int32 [32768], P(('scene', 'scat')), parts along dimension 0, may hold values 0 or 1
- stolt_block: int32 [512, 32], P(('pulse', 'scat')), may hold values from 0 to 30
- kernel_choice: int32 [512, 32], P(('pulse', 'scat')), may hold values from 0 to 15
- kernel_bank: float32 [16, 256, 128], replicated, may hold values from -0.375 to 0.375
Outputs:
- image: float32 [2, 1024, 4096], P(None, 'scene', ('pulse', 'scat')), parts along dimension 1
There are 2 independent parts, one for each index of `scene`. A program takes and returns all parts, laid end to end along the dimension named above; an argument that names none is the same for every part. Nothing has to cross between parts.
All inputs are finite; a program needn't handle non-finite values. No bound on the sum of `bounce` on one device may be relied on, other than what follows from the above.
Results may differ from a plain program's by a relative error of at most 0.0003.
Values sent between devices are 32-bit elements; how exact they have to be, the bound alone decides.
A program may use at most 64 MiB of HBM per device.

v0:
```python
import functools

import jax
import jax.numpy as jnp
import numpy as np
from jax import lax
from jax.experimental import pallas as pl
from jax.experimental.pallas import tpu as pltpu
from jax.sharding import PartitionSpec as P

P_SIZE = 512
F_LEN = 4096
B = 1024
SHIFT = 16
STOLT = 128
BLOCKS = 32
SPACING = 2.0
NEAR = 700000.0
BIN_SIDE = 32
GROUP = 4
HIGH = lax.Precision.HIGH
f32 = jnp.float32
bf16 = jnp.bfloat16


def trig_coefs():
    x = np.cos(np.pi * (np.arange(400) + 0.5) / 400) * 0.5
    u = x * x
    s = np.polynomial.chebyshev.Chebyshev.fit(u, np.sin(np.pi * x) / x, 5).convert(
        kind=np.polynomial.Polynomial
    )
    c = np.polynomial.chebyshev.Chebyshev.fit(u, np.cos(np.pi * x), 5).convert(
        kind=np.polynomial.Polynomial
    )
    return [float(v) for v in s.coef], [float(v) for v in c.coef]


def horner(u, coefs):
    acc = jnp.full_like(u, coefs[-1])
    for c in coefs[-2::-1]:
        acc = acc * u + c
    return acc


def split(x):
    hi = x.astype(bf16)
    lo = (x - hi.astype(f32)).astype(bf16)
    return hi, lo


def np_split(x):
    x = np.asarray(x, np.float64)
    hi = np.asarray(x, jnp.bfloat16)
    lo = np.asarray(x - hi.astype(np.float64), jnp.bfloat16)
    return np.stack([hi, lo])


def dots(a, b, dims):
    d = functools.partial(
        lax.dot_general, dimension_numbers=(dims, ((), ())), preferred_element_type=f32
    )
    return d(a[0], b[0]) + (d(a[0], b[1]) + d(a[1], b[0]))


def bin_kernel(pulse_base, pos, amp, tgt, bnc, out, acc, *, pulses, sin_c, cos_c):
    step = pl.program_id(0)
    width = pos.shape[1]

    @pl.when(step == 0)
    def _():
        acc[...] = jnp.zeros_like(acc)

    base = pulse_base[0]
    ids = base + lax.broadcasted_iota(jnp.int32, (pulses, width), 0)
    along = (ids.astype(f32) - P_SIZE // 2) * SPACING
    target = tgt[...] + SHIFT * bnc[...]
    slant = NEAR + target.astype(f32)
    offset = along - pos[...]
    square = offset * offset
    excess = square / (jnp.sqrt(slant * slant + square) + slant)
    halves = excess * -128.0
    whole = jnp.round(halves)
    r = halves - whole
    u = r * r
    odd = whole - 2.0 * jnp.floor(whole * 0.5)
    sign = 1.0 - 2.0 * odd
    sin_p = sign * r * horner(u, sin_c)
    cos_p = sign * horner(u, cos_c)
    flip = 1.0 - 2.0 * bnc[...].astype(f32)
    are = flip * amp[0:1]
    aim = flip * amp[1:2]
    re = are * cos_p - aim * sin_p
    im = are * sin_p + aim * cos_p
    steer = jnp.concatenate([re, im], 0)
    hi, lo = split(steer)
    rhs = jnp.concatenate([hi, lo], 0)
    bins = lax.broadcasted_iota(jnp.int32, (B, width), 0)
    hot = jnp.where(bins == target, 1.0, 0.0).astype(bf16)
    acc[...] += lax.dot_general(
        hot, rhs, (((1,), (1,)), ((), ())), preferred_element_type=f32
    )

    @pl.when(step == pl.num_programs(0) - 1)
    def _():
        out[...] = acc[:, : 2 * pulses] + acc[:, 2 * pulses :]


def binning(positions, amplitude, cells, bounce, pulse_base, pulses):
    count = positions.shape[0]
    width = min(2048, count)
    sin_c, cos_c = trig_coefs()
    row = lambda n: pl.BlockSpec((n, width), lambda i: (0, i))
    return pl.pallas_call(
        functools.partial(bin_kernel, pulses=pulses, sin_c=sin_c, cos_c=cos_c),
        grid=(count // width,),
        in_specs=[pl.BlockSpec(memory_space=pltpu.SMEM), row(1), row(2), row(1), row(1)],
        out_specs=pl.BlockSpec((B, 2 * pulses), lambda i: (0, 0)),
        out_shape=jax.ShapeDtypeStruct((B, 2 * pulses), f32),
        scratch_shapes=[pltpu.VMEM((B, 4 * pulses), f32)],
        name="binning",
    )(
        pulse_base.reshape(1),
        positions.reshape(1, count),
        amplitude,
        cells.reshape(1, count),
        bounce.reshape(1, count),
    )


def complex_rows(c, s):
    return np.block([[c, s], [-s, c]])


def mid_tables(n_dev, order):
    side = np.arange(BIN_SIDE)
    t = np.arange(STOLT)
    eye = np.eye(GROUP)
    a = -2 * np.pi / STOLT * ((side[:, None] * t[None, :]) % STOLT)
    ta = complex_rows(np.cos(a), np.sin(a))[order]
    a = -2 * np.pi / F_LEN * (side[:, None] * t[None, :])
    wa = np.stack([np.tile(np.cos(a), (GROUP, 1)), np.tile(np.sin(a), (GROUP, 1))])
    a = -2 * np.pi / BIN_SIDE * ((side[:, None] * side[None, :]) % BIN_SIDE)
    c, s = np.kron(eye, np.cos(a)), np.kron(eye, np.sin(a))
    tb = complex_rows(c, s).T
    blk = np.arange(BLOCKS)
    a = 2 * np.pi / BLOCKS * ((blk[:, None] * blk[None, :]) % BLOCKS)
    c, s = np.kron(eye, np.cos(a)), np.kron(eye, np.sin(a))
    tc = complex_rows(c, s)
    a = 2 * np.pi / F_LEN * (t[:, None] * blk[None, :])
    wc = np.stack([np.tile(np.cos(a), (1, GROUP)), np.tile(np.sin(a), (1, GROUP))])
    a = 2 * np.pi / STOLT * ((t[:, None] * t[None, :]) % STOLT)
    td = complex_rows(np.cos(a), np.sin(a)).T / F_LEN
    td = td.reshape(2, n_dev, STOLT // n_dev, 2 * STOLT).transpose(1, 0, 2, 3)
    td = td.reshape(2 * STOLT, 2 * STOLT)
    return (
        np_split(ta),
        wa.astype(np.float32),
        np_split(tb),
        np_split(tc),
        wc.astype(np.float32),
        np_split(td),
    )


def mid_kernel(
    x, cos_p, sin_p, hot, kind, bank_hi, bank_lo, ta, wa, tb, tc, wc, td, out, xs, os, *, subs
):
    n = GROUP * BLOCKS
    step = pl.program_id(0)
    groups = x.shape[1]

    @pl.when(step == 0)
    def _():
        for g in range(groups):
            xs[g] = x[:, g, :]

    parts_hi, parts_lo = [], []
    for g in range(subs):
        lanes = slice(g * n, (g + 1) * n)
        y = dots(split(xs[step * subs + g]), (ta[0], ta[1]), ((0,), (0,)))
        yr, yi = y[:, :STOLT], y[:, STOLT:]
        y = jnp.concatenate([yr * wa[0] - yi * wa[1], yr * wa[1] + yi * wa[0]], 0)
        z = dots((tb[0], tb[1]), split(y), ((1,), (0,)))
        zr, zi = z[:n], z[n:]
        cp, sp = cos_p[lanes], sin_p[lanes]
        z = jnp.concatenate([zr * cp - zi * sp, zr * sp + zi * cp], 1)
        hi, lo = split(z)
        picked = jnp.dot(
            hot[g], jnp.concatenate([hi, lo], 1), preferred_element_type=f32
        ).astype(bf16)
        first, second = picked[:n], picked[n:]
        for c in range(2):
            for base, keep in ((0, parts_hi), (2 * STOLT, parts_lo)):
                cut = slice(base + c * STOLT, base + (c + 1) * STOLT)
                keep.append(jnp.concatenate([first[:, cut], second[:, cut]], 1))
    ghi = jnp.concatenate(parts_hi, 0)
    glo = jnp.concatenate(parts_lo, 0)
    kinds = kind[...].reshape(subs * 2 * n, 1)
    kinds = jnp.broadcast_to(kinds, (subs * 2 * n, STOLT))
    acc = jnp.zeros((subs * 2 * n, STOLT), f32)
    for k in range(0, bank_hi.shape[0], 2):
        khi = jnp.concatenate([bank_hi[k], bank_hi[k + 1]], 1)
        klo = jnp.concatenate([bank_lo[k], bank_lo[k + 1]], 1)
        r = dots((ghi, glo), (khi, klo), ((1,), (0,)))
        for half in range(2):
            acc = jnp.where(kinds == k + half, r[:, half * STOLT : (half + 1) * STOLT], acc)
    for g in range(subs):
        s = acc[g * 2 * n : (g + 1) * 2 * n]
        y = dots(split(s), (tc[0], tc[1]), ((0,), (0,)))
        yr, yi = y[:, :n], y[:, n:]
        y = jnp.concatenate([yr * wc[0] - yi * wc[1], yr * wc[1] + yi * wc[0]], 0)
        os[step * subs + g] = dots((td[0], td[1]), split(y), ((1,), (0,)))

    @pl.when(step == pl.num_programs(0) - 1)
    def _():
        for g in range(groups):
            out[:, g, :] = os[g]


def middle(x, cos_p, sin_p, hot, kind, bank_hi, bank_lo, tables):
    groups = x.shape[1]
    subs = min(4, groups)
    n = GROUP * BLOCKS
    whole = lambda a: pl.BlockSpec(a.shape, lambda i: (0,) * a.ndim)
    return pl.pallas_call(
        functools.partial(mid_kernel, subs=subs),
        grid=(groups // subs,),
        in_specs=[
            whole(x),
            pl.BlockSpec((subs * n, STOLT), lambda i: (i, 0)),
            pl.BlockSpec((subs * n, STOLT), lambda i: (i, 0)),
            pl.BlockSpec((subs, 2 * n, n), lambda i: (i, 0, 0)),
            pl.BlockSpec((subs, 2 * n, 1), lambda i: (i, 0, 0)),
            whole(bank_hi),
            whole(bank_lo),
        ]
        + [whole(t) for t in tables],
        out_specs=pl.BlockSpec((2 * STOLT, groups, n), lambda i: (0, 0, 0)),
        out_shape=jax.ShapeDtypeStruct((2 * STOLT, groups, n), f32),
        scratch_shapes=[
            pltpu.VMEM((groups, x.shape[0], n), f32),
            pltpu.VMEM((groups, 2 * STOLT, n), f32),
        ],
        name="middle",
    )(x, cos_p, sin_p, hot, kind, bank_hi, bank_lo, *tables)


def quarter_tables():
    q = P_SIZE // 4
    m = np.arange(q)
    fwd, inv = [], []
    for low in range(4):
        a = 2 * np.pi / P_SIZE * (((4 * m[:, None] + low) * m[None, :]) % P_SIZE)
        fwd.append(np.concatenate([np.cos(a), np.sin(a)], 0))
        inv.append(np.concatenate([np.cos(a.T), np.sin(a.T)], 0) / P_SIZE)
    return np_split(np.stack(fwd)), np_split(np.stack(inv))


def swap_blocks(arrays):
    count = len(arrays)
    lanes = arrays[0].shape[-1]
    size = lanes // count
    block = lax.broadcasted_iota(jnp.int32, arrays[0].shape, 1) // size
    outs = []
    for b in range(count):
        acc = None
        for a in range(count):
            shift = (a - b) % count * size
            moved = pltpu.roll(arrays[a], shift, 1) if shift else arrays[a]
            acc = moved if acc is None else jnp.where(block == a, moved, acc)
        outs.append(acc)
    return outs


def azimuth_kernel(x, table, out):
    srcs, bins, lanes = x.shape
    half = lanes // 2
    low = lax.broadcasted_iota(jnp.int32, (bins, lanes), 1) < half
    quarters = []
    for q in range(4):
        a, b = x[2 * q], x[2 * q + 1]
        re = jnp.where(low, a, pltpu.roll(b, half, 1))
        im = jnp.where(low, pltpu.roll(a, half, 1), b)
        quarters.append((re, im))
    (r0, i0), (r1, i1), (r2, i2), (r3, i3) = quarters
    sr, si, dr, di = r0 + r2, i0 + i2, r0 - r2, i0 - i2
    tr, ti, er, ei = r1 + r3, i1 + i3, r1 - r3, i1 - i3
    mixed = (
        (sr + tr, si + ti),
        (dr + ei, di - er),
        (sr - tr, si - ti),
        (dr - ei, di + er),
    )
    size = P_SIZE // 4
    low = lax.broadcasted_iota(jnp.int32, (size, lanes), 1) < half
    rows = []
    for k in range(4):
        u = jnp.concatenate(mixed[k], 0)
        g = dots((table[0, k], table[1, k]), split(u), ((1,), (1,)))
        turned = pltpu.roll(g[size:], half, 1)
        rows.append(g[:size] + jnp.where(low, turned, -turned))
    for q, z in enumerate(swap_blocks(rows)):
        out[:, q] = z.reshape(out.shape[0], out.shape[2], lanes)


def image_kernel(x, table, out):
    devs, _, per, kh, lanes = x.shape
    size = P_SIZE // 4
    columns = [[] for _ in range(4)]
    for c in range(2):
        for h in range(per // 4):
            tiles = [x[:, c, 4 * h + j].reshape(devs * kh, lanes) for j in range(4)]
            for k, z in enumerate(swap_blocks(tiles)):
                columns[k].append(z)
    width = lanes * (per // 4)
    v = []
    for k in range(4):
        g = dots((table[0, k], table[1, k]), split(jnp.concatenate(columns[k], 1)), ((1,), (0,)))
        cos_g, sin_g = g[:size], g[size:]
        v.append((cos_g[:, :width] - sin_g[:, width:], cos_g[:, width:] + sin_g[:, :width]))
    (r0, i0), (r1, i1), (r2, i2), (r3, i3) = v
    sr, si, dr, di = r0 + r2, i0 + i2, r0 - r2, i0 - i2
    tr, ti, er, ei = r1 + r3, i1 + i3, r1 - r3, i1 - i3
    mixed = (
        (sr + tr, si + ti),
        (dr - ei, di + er),
        (sr - tr, si - ti),
        (dr + ei, di - er),
    )
    for q in range(4):
        for c in range(2):
            out[c, q * size : (q + 1) * size, :] = mixed[q][c]


def reference_phase(row_ids, cols):
    centered = (row_ids + P_SIZE // 2) % P_SIZE - P_SIZE // 2
    along_k = 2.0 * jnp.pi / (P_SIZE * SPACING) * centered.astype(f32)
    kr = 4.0 * jnp.pi / 3e8 * (9.6e9 + (cols.astype(f32) - F_LEN // 2) * (1.5e8 / F_LEN))
    squared = along_k * along_k
    depth = NEAR + B // 2
    return (
        -depth
        * squared[:, None]
        / (jnp.sqrt(kr[None, :] * kr[None, :] - squared[:, None]) + kr[None, :])
    )


def on_device(positions, amplitude, range_cells, bounce, stolt_block, kernel_choice, kernel_bank):
    n_pulse = lax.axis_size("pulse")
    n_scat = lax.axis_size("scat")
    n_dev = n_pulse * n_scat
    pulse_here = lax.axis_index("pulse")
    scat_here = lax.axis_index("scat")
    pulses = P_SIZE // n_pulse
    rows = P_SIZE // n_dev
    width = F_LEN // n_dev
    groups = rows // GROUP
    n = GROUP * BLOCKS
    bins_scat = B // n_scat
    bins_here = bins_scat // n_pulse

    ids = jnp.arange(GROUP, dtype=jnp.int32)[None, :, None] * BLOCKS
    first = stolt_block.reshape(groups, GROUP, BLOCKS) + ids
    pick = jnp.stack([first, first + 1], 1).reshape(groups, 2 * n, 1)
    hot = (pick == jnp.arange(n, dtype=jnp.int32)[None, None, :]).astype(bf16)
    kind = jnp.stack([kernel_choice.reshape(groups, n)] * 2, 1).reshape(groups, 2 * n, 1)
    bank_hi = lax.reduce_precision(kernel_bank, 8, 7)
    bank_lo = (kernel_bank - bank_hi).astype(bf16)
    bank_hi = bank_hi.astype(bf16)
    row_ids = (pulse_here * n_scat + scat_here) * rows + jnp.arange(rows, dtype=jnp.int32)
    theta = reference_phase(row_ids, jnp.arange(F_LEN, dtype=jnp.int32))
    theta = theta.reshape(rows * BLOCKS, STOLT)
    cos_p, sin_p = jnp.cos(theta), jnp.sin(theta)

    partial = binning(positions, amplitude, range_cells, bounce, pulse_here * pulses, pulses)
    partial = partial.reshape(n_scat, bins_scat, 2 * pulses)
    binned = lax.dynamic_index_in_dim(partial, scat_here, 0, keepdims=False)
    for shift in range(1, n_scat):
        other = lax.dynamic_index_in_dim(
            partial, (scat_here + shift) % n_scat, 0, keepdims=False
        )
        ring = [(i, (i + shift) % n_scat) for i in range(n_scat)]
        binned = binned + lax.ppermute(other, "scat", ring)

    turned = lax.all_to_all(
        binned.reshape(n_pulse, bins_here, 2 * pulses), "pulse", 0, 0, tiled=True
    )
    per = STOLT // n_dev
    packed = 2 * pulses == 128 and 2 * bins_here == 128 and per % 4 == 0 and groups % 8 == 0
    if packed:
        forward, backward = (jnp.asarray(t) for t in quarter_tables())
        spectrum = pl.pallas_call(
            azimuth_kernel,
            out_shape=jax.ShapeDtypeStruct((n_dev, 4, groups, n), f32),
            name="azimuth",
        )(turned, forward)
        x = lax.all_to_all(spectrum, ("pulse", "scat"), 0, 0, tiled=True)
        x = x.reshape(4 * n_dev, groups, n)
        local = bins_here // BIN_SIDE
        i, s, c, l = np.meshgrid(
            np.arange(n_pulse), np.arange(n_scat), np.arange(2), np.arange(local), indexing="ij"
        )
        order = (c * BIN_SIDE + s * (BIN_SIDE // n_scat) + i * local + l).reshape(-1)
    else:
        turned = turned.reshape(n_pulse, bins_here, 2, pulses).transpose(0, 3, 2, 1)
        turned = turned.reshape(P_SIZE, 2 * bins_here)
        k = np.arange(P_SIZE)
        angle = 2 * np.pi / P_SIZE * ((k[:, None] * k[None, :]) % P_SIZE)
        az = jnp.asarray(np.concatenate([np.cos(angle), np.sin(angle)], 0), f32)
        product = jnp.dot(az, turned, precision=HIGH, preferred_element_type=f32)
        pc, ps = product[:P_SIZE], product[P_SIZE:]
        spectrum = pc + jnp.concatenate([ps[:, bins_here:], -ps[:, :bins_here]], 1)
        az_rows = lax.all_to_all(
            spectrum.reshape(n_dev, rows, 2 * bins_here), ("pulse", "scat"), 0, 0, tiled=True
        )
        x = az_rows.reshape(n_pulse, n_scat, rows, 2, bins_here).transpose(3, 1, 0, 4, 2)
        x = x.reshape(2, BIN_SIDE, BIN_SIDE, rows).transpose(0, 1, 3, 2)
        x = x.reshape(2 * BIN_SIDE, groups, n)
        order = np.arange(2 * BIN_SIDE)

    tables = tuple(jnp.asarray(t) for t in mid_tables(n_dev, order))
    ranged = middle(x, cos_p, sin_p, hot, kind, bank_hi, bank_lo, tables)
    if packed:
        columns = lax.all_to_all(
            ranged.reshape(n_dev, 2, per, groups, n), ("pulse", "scat"), 0, 0, tiled=True
        )
        return pl.pallas_call(
            image_kernel,
            out_shape=jax.ShapeDtypeStruct((2, P_SIZE, width), f32),
            name="image",
        )(columns, backward)
    columns = lax.all_to_all(
        ranged.reshape(n_dev, 2 * per, rows * BLOCKS), ("pulse", "scat"), 0, 0, tiled=True
    )
    columns = columns.reshape(n_dev, 2, per, rows, BLOCKS).transpose(0, 3, 1, 2, 4)
    columns = columns.reshape(P_SIZE, 2 * width)
    final = jnp.dot(az, columns, precision=HIGH, preferred_element_type=f32)
    fc, fs = final[:P_SIZE], final[P_SIZE:]
    re = (fc[:, :width] - fs[:, width:]) / P_SIZE
    im = (fc[:, width:] + fs[:, :width]) / P_SIZE
    return jnp.stack([re, im])


def solution(mesh):
    placed = (
        P(("scene", "scat")),
        P(None, ("scene", "scat")),
        P(("scene", "scat")),
        P(("scene", "scat")),
        P(("pulse", "scat"), None),
        P(("pulse", "scat"), None),
        P(),
    )
    return jax.shard_map(
        on_device,
        mesh=mesh,
        in_specs=placed,
        out_specs=P(None, "scene", ("pulse", "scat")),
        check_vma=False,
    )
```

profile of v0, /device:TPU:0, one launch (start us, length us, event | category | flops | bytes accessed | tf_op | source)
XLA Modules:
  0.0 100.5 jit_solution(9468694765716790324)
XLA Ops:
  0.0 0.0 copy-start.3
  0.0 10.2 %binning.1 = f32[1024,128]{1,0:T(8,128)} custom-call(s32[1]{0:T(128)} %bitcast.pulse_base, f32[1,8192]{1,0:T(1,128)} %bitcast.37, f32[2,8192]{1,0:T(2,128)} %amp.1, s32[1,8192]{1,0:T(1,128)} %bitcast.38, s32[1,8192]{1,0:T(1,128)} %bitcast.39), custom_call_target="tpu_custom_call" | custom-call | tf_op jit(solution)/shard_map/binning/pallas_call | solution.py:113
  10.2 1.0 dynamic-slice_bitcast_fusion
  11.1 0.6 collective-permute-start
  11.7 0.8 stack_reshape.4
  12.5 0.1 sub.36
  12.6 0.1 sub.37
  12.6 0.1 div.13
  12.7 0.1 div.14
  12.8 0.1 collective-permute-done
  12.8 1.7 %bitcast_add_fusion.1 = f32[512,128]{1,0:T(8,128)} fusion(f32[512,128]{1,0:T(8,128)S(1)} %collective-permute-done, f32[2,512,128]{2,1,0:T(8,128)} %bitcast.35, s32[]{:T(128)S(6)} %select_n.27), kind=kLoop, calls=%fused_computation.11 | loop fusion | flops 65536 | bytes 786436 | tf_op jit(solution)/shard_map/add | solution.py:383
  14.5 7.2 %all-to-all-start = ((f32[8,64,128]{2,1,0:T(8,128)}), f32[8,64,128]{2,1,0:T(8,128)S(1)}, u32[]{:S(2)}, u32[]{:S(2)}) async-start(f32[8,64,128]{2,1,0:T(8,128)} %bitcast.7), calls=%async_computation | async-start | bytes 524288 | tf_op jit(solution)/shard_map/all_to_all | solution.py:385
  21.7 0.0 copy-done.3
  21.7 0.1 broadcast_add_fusion
  21.8 0.1 eq.19
  21.9 0.0 copy-start
  21.9 1.3 %copy.20.kind = s32[8,256,1]{2,1,0:T(8,128)} copy(s32[8,256,1]{1,0,2:T(8,128)S(1)} %add_bitcast_fusion) | data formatting | bytes 16384 | tf_op jit(solution)/shard_map/reshape | solution.py:366
  23.2 3.6 %fusion.4 = (f32[1024,128]{1,0:T(8,128)}, f32[1024,128]{1,0:T(8,128)}) fusion(f32[32,128]{1,0:T(8,128)S(1)} %get-tuple-element.13, f32[1024]{0:T(1024)S(1)} %sub.37, f32[32,128]{1,0:T(8,128)S(1)} %get-tuple-element.14, f32[1024]{0:T(1024)S(1)} %div.14), kind=kLoop, calls=%fused_computation.9 | loop fusion | flops 393216 | bytes 1089536 | tf_op jit(solution)/shard_map/sin | solution.py:373
  26.8 4.1 %all-to-all-done.x = f32[8,64,128]{2,1,0:T(8,128)S(1)} async-done(((f32[8,64,128]{2,1,0:T(8,128)}), f32[8,64,128]{2,1,0:T(8,128)S(1)}, u32[]{:S(2)}, u32[]{:S(2)}) %all-to-all-start) | async-done | bytes 262176 | tf_op jit(solution)/shard_map/all_to_all | solution.py:385
  30.9 0.0 copy-start.2
  30.9 0.7 copy-done.2
  31.6 2.6 %azimuth.1 = f32[16,4,8,128]{3,2,1,0:T(8,128)} custom-call(f32[8,64,128]{2,1,0:T(8,128)} %copy-done.2, bf16[2,4,256,128]{3,2,1,0:T(8,128)(2,1)} %constant.82.clone.table), custom_call_target="tpu_custom_call" | custom-call | tf_op jit(solution)/shard_map/azimuth/pallas_call | solution.py:392
  34.2 3.7 %all-to-all-start.1 = ((f32[16,4,8,128]{3,2,1,0:T(8,128)}), f32[16,4,8,128]{3,2,1,0:T(8,128)S(1)}, u32[]{:S(2)}, u32[]{:S(2)}) async-start(f32[16,4,8,128]{3,2,1,0:T(8,128)} %azimuth.1), calls=%async_computation.1 | async-start | bytes 524288 | tf_op jit(solution)/shard_map/all_to_all | solution.py:397
  37.9 1.1 %fusion.1.hot = bf16[8,256,128]{2,1,0:T(8,128)(2,1)} fusion(s32[8,256]{1,0:T(8,128)S(1)} %eq.19), kind=kLoop, calls=%fused_computation.4 | loop fusion | flops 524288 | bytes 532480 | tf_op jit(solution)/shard_map/convert_element_type | solution.py:365
  39.0 0.0 copy-done
  39.0 1.9 %fusion = (bf16[16,256,128]{2,1,0:T(8,128)(2,1)}, bf16[16,256,128]{2,1,0:T(8,128)(2,1)}) fusion(f32[16,256,128]{2,1,0:T(8,128)S(1)} %copy-done), kind=kLoop, calls=%fused_computation.2 | loop fusion | flops 2097152 | bytes 4194304 | tf_op jit(solution)/shard_map/convert_element_type | solution.py:368
  40.9 7.0 %all-to-all-done.1 = f32[16,4,8,128]{3,2,1,0:T(8,128)S(1)} async-done(((f32[16,4,8,128]{3,2,1,0:T(8,128)}), f32[16,4,8,128]{3,2,1,0:T(8,128)S(1)}, u32[]{:S(2)}, u32[]{:S(2)}) %all-to-all-start.1) | async-done | bytes 262176 | tf_op jit(solution)/shard_map/all_to_all | solution.py:397
  47.9 0.0 copy-start.1
  47.9 0.7 copy-done.1
  48.6 19.2 %middle.1 = f32[256,8,128]{2,1,0:T(8,128)} custom-call(f32[64,8,128]{2,1,0:T(8,128)} %bitcast.36, f32[1024,128]{1,0:T(8,128)} %get-tuple-element.10.cos_p, f32[1024,128]{1,0:T(8,128)} %get-tuple-element.9.sin_p, bf16[8,256,128]{2,1,0:T(8,128)(2,1)} %fusion.1.hot, s32[8,256,1]{2,1,0:T(8,128)} %copy.20.kind, bf16[16,256,128]{2,1,0:T(8,128)(2,1)} %get-tuple-element.8.bank_hi, ...), custom_call_target="tpu_custom_call" | custom-call | tf_op jit(solution)/shard_map/middle/pallas_call | solution.py:225
  67.8 29.0 %all_to_all.15.x = f32[16,2,8,8,128]{4,3,2,1,0:T(8,128)} all-to-all(f32[16,2,8,8,128]{4,3,2,1,0:T(8,128)} %bitcast.33), channel_id=1, replica_groups=mesh['scene'=2,'pulse'=8,'scat'=2] {'pulse','scat'}, dimensions={0} | all-to-all | bytes 2097152 | tf_op jit(solution)/shard_map/all_to_all | solution.py:424
  96.8 3.7 %image.1 = f32[2,512,256]{2,1,0:T(8,128)} custom-call(f32[16,2,8,8,128]{4,3,2,1,0:T(8,128)} %all_to_all.15.x, bf16[2,4,256,128]{3,2,1,0:T(8,128)(2,1)} %constant.83.clone.table), custom_call_target="tpu_custom_call" | custom-call | tf_op jit(solution)/shard_map/image/pallas_call | solution.py:427
  (6 shorter events, 0.1 us)
Async XLA Ops:
  0.0 21.7 %copy-start.3 = (s32[32,32]{1,0:T(8,128)S(1)}, s32[32,32]{1,0:T(8,128)}, u32[]{:S(2)}) copy-start(s32[32,32]{1,0:T(8,128)} %param.19) | copy-start | bytes 12292
  11.1 1.7 %collective-permute-start = (f32[512,128]{1,0:T(8,128)S(1)}, f32[512,128]{1,0:T(8,128)S(1)}, u32[]{:S(2)}, u32[]{:S(2)}) collective-permute-start(f32[512,128]{1,0:T(8,128)S(1)} %dynamic-slice_bitcast_fusion), channel_id=1, source_target_pairs={{0,1},{1,0},{2,3},{3,2},{4,5},{5,4},{6,7},{7,6},{8,9},{9,8},{10,11... | collective-permute-start | bytes 786440 | tf_op jit(solution)/shard_map/ppermute | solution.py:383
  14.5 16.4 %all-to-all-start = ((f32[8,64,128]{2,1,0:T(8,128)}), f32[8,64,128]{2,1,0:T(8,128)S(1)}, u32[]{:S(2)}, u32[]{:S(2)}) async-start(f32[8,64,128]{2,1,0:T(8,128)} %bitcast.7), calls=%async_computation | async-start | bytes 524288 | tf_op jit(solution)/shard_map/all_to_all | solution.py:385
  21.9 17.1 %copy-start = (f32[16,256,128]{2,1,0:T(8,128)S(1)}, f32[16,256,128]{2,1,0:T(8,128)}, u32[]{:S(2)}) copy-start(f32[16,256,128]{2,1,0:T(8,128)} %param.21) | copy-start | bytes 6291460
  30.9 0.7 copy-start.2
  34.2 13.7 %all-to-all-start.1 = ((f32[16,4,8,128]{3,2,1,0:T(8,128)}), f32[16,4,8,128]{3,2,1,0:T(8,128)S(1)}, u32[]{:S(2)}, u32[]{:S(2)}) async-start(f32[16,4,8,128]{3,2,1,0:T(8,128)} %azimuth.1), calls=%async_computation.1 | async-start | bytes 524288 | tf_op jit(solution)/shard_map/all_to_all | solution.py:397
  47.9 0.7 copy-start.1
where the time goes:
time: 102 us; the launch traced here: 101 us
  Pallas kernels  35.7 us (35%)
  blocking collectives  29 us (28%)
  starting transfers between devices  11.4 us (11%)
  waiting for transfers between devices  11.2 us (11%)
  other arithmetic  8.36 us (8%)
  local copies, waits for them, and re-layouts  4.9 us (5%)
    all_to_all x1, blocking collectives, on_device(): lax.all_to_all(ranged.reshape(n_dev, 2, per, groups, n), ('pulse', 'scat'...  29 us
    pallas_call x1, Pallas kernels, middle(): pl.pallas_call(functools.partial(mid_kernel, subs=subs), grid=(groups //...  19.2 us
    pallas_call x1, Pallas kernels, binning(): pl.pallas_call(functools.partial(bin_kernel, pulses=pulses, sin_c=sin_c,...  10.2 us
    all_to_all x1, starting transfers between devices, on_device(): lax.all_to_all(binned.reshape(n_pulse, bins_here, 2 * pulses), 'pulse', 0...  7.16 us
    all_to_all x1, waiting for transfers between devices, on_device(): x = lax.all_to_all(spectrum, ('pulse', 'scat'), 0, 0, tiled=True)  7.03 us
    all_to_all x1, waiting for transfers between devices, on_device(): lax.all_to_all(binned.reshape(n_pulse, bins_here, 2 * pulses), 'pulse', 0...  4.07 us
    pallas_call x1, Pallas kernels, on_device(): pl.pallas_call(image_kernel, out_shape=jax.ShapeDtypeStruct((2, P_SIZE, w...  3.74 us
    all_to_all x1, starting transfers between devices, on_device(): x = lax.all_to_all(spectrum, ('pulse', 'scat'), 0, 0, tiled=True)  3.69 us
  transfers between devices with their start and end apart: 3, of which 3 were waited for; matrix products, arithmetic and copies ran while one was open for 9% of the time, Pallas kernels for 0%

commit v1 on v0

--- a/solution.py
+++ b/solution.py
@@ -18,6 +18,9 @@
 NEAR = 700000.0
 BIN_SIDE = 32
 GROUP = 4
+CHUNK = 1024
+SLOTS = 192
+WIDE = 256
 HIGH = lax.Precision.HIGH
 f32 = jnp.float32
 bf16 = jnp.bfloat16
@@ -120,6 +123,157 @@
         name="binning",
     )(
         pulse_base.reshape(1),
+        positions.reshape(1, count),
+        amplitude,
+        cells.reshape(1, count),
+        bounce.reshape(1, count),
+    )
+
+
+def range_trig_coefs(degree):
+    x = np.cos(np.pi * (np.arange(400) + 0.5) / 400) * 0.5
+    u = x * x
+    fit = lambda y: np.polynomial.chebyshev.Chebyshev.fit(u, y, degree).convert(
+        kind=np.polynomial.Polynomial
+    )
+    return [float(v) for v in fit(np.sin(np.pi * x) / x).coef], [
+        float(v) for v in fit(np.cos(np.pi * x)).coef
+    ]
+
+
+def split3(x):
+    hi = x.astype(bf16).astype(f32)
+    rest = x - hi
+    mid = rest.astype(bf16).astype(f32)
+    return hi, mid, rest - mid
+
+
+def range_bin_kernel(
+    base_ref, cells8, bounce8, pos, amp, cells, bnc, out, buf, acc, *, span, sin_c, cos_c
+):
+    base = base_ref[0]
+    rows = cells8.shape[0]
+    chunks = rows // 8
+    target = cells8[...] + SHIFT * bounce8[...] - base
+    match = jnp.where((target >= 0) & (target < span), 1.0, 0.0)
+    mb = match.astype(bf16)
+    a = lax.broadcasted_iota(jnp.int32, (128, 128), 0)
+    b = lax.broadcasted_iota(jnp.int32, (128, 128), 1)
+    upto = jnp.where(a <= b, 1.0, 0.0).astype(bf16)
+    count = jnp.dot(mb, upto, preferred_element_type=f32)
+    total = jnp.dot(mb, jnp.ones((128, 128), bf16), preferred_element_type=f32)
+    a = lax.broadcasted_iota(jnp.int32, (rows, rows), 0)
+    b = lax.broadcasted_iota(jnp.int32, (rows, rows), 1)
+    below = jnp.where((a // 8 == b // 8) & (b < a), 1.0, 0.0).astype(bf16)
+    ahead = jnp.dot(below, total.astype(bf16), preferred_element_type=f32)
+    rank = jnp.where(match > 0.0, count + ahead - 1.0, -1.0)
+    counts = [
+        jnp.sum(match[8 * c : 8 * c + 8]).astype(jnp.int32) for c in range(chunks)
+    ]
+
+    def values(c):
+        lanes = slice(CHUNK * c, CHUNK * (c + 1))
+        flip = 1.0 - 2.0 * bnc[:, lanes].astype(f32)
+        rel = (cells[:, lanes] + SHIFT * bnc[:, lanes] - base).astype(f32)
+        zero = jnp.zeros_like(rel)
+        data = jnp.concatenate(
+            [pos[:, lanes], amp[0:1, lanes] * flip, amp[1:2, lanes] * flip, rel] + [zero] * 4, 0
+        )
+        return jnp.concatenate(list(split3(data)) + [jnp.zeros_like(data)], 0).astype(bf16)
+
+    def pick(c, first):
+        slots = lax.broadcasted_iota(jnp.int32, (SLOTS, 128), 0).astype(f32) + first
+        hot = jnp.concatenate(
+            [jnp.where(rank[8 * c + j : 8 * c + j + 1] == slots, 1.0, 0.0) for j in range(8)], 1
+        ).astype(bf16)
+        return lax.dot_general(
+            hot, values(c), (((1,), (1,)), ((), ())), preferred_element_type=f32
+        )
+
+    start = 0
+    for c in range(chunks):
+        buf[pl.ds(start, SLOTS), 0:32] = pick(c, 0.0)
+        start = start + counts[c]
+    most = functools.reduce(jnp.maximum, counts)
+
+    @pl.when(most > SLOTS)
+    def _():
+        begin = 0
+        for c in range(chunks):
+
+            @pl.loop(0, (counts[c] + SLOTS - 1) // SLOTS)
+            def _(i):
+                first = (i * SLOTS).astype(f32)
+                buf[pl.ds(begin + i * SLOTS, SLOTS), 0:32] = pick(c, first)
+
+            begin = begin + counts[c]
+
+    buf[pl.ds(start, WIDE), :] = jnp.zeros((WIDE, 128), f32)
+    acc[...] = jnp.zeros_like(acc)
+    bins = lax.broadcasted_iota(jnp.int32, (span, WIDE), 0).astype(f32)
+    nearest = base.astype(f32) + NEAR
+
+    @pl.loop(0, (start + WIDE - 1) // WIDE)
+    def _(i):
+        cols = []
+        for h in range(WIDE // 128):
+            t = buf[pl.ds(i * WIDE + h * 128, 128), :].T
+            cols.append(t[0:8] + t[8:16] + t[16:24])
+        data = jnp.concatenate(cols, 1)
+        where, re_amp, im_amp, rel = (data[j : j + 1] for j in range(4))
+        re2, im2 = 2.0 * re_amp, 2.0 * im_amp
+        inverse = 0.5 / (rel + nearest)
+        gain = inverse * -64.0
+        bend = inverse * (1.0 / 64.0)
+        hot = jnp.where(bins == rel, 1.0, 0.0).astype(bf16)
+        for q in range(P_SIZE // 128):
+            parts = []
+            for p in range(0, 128, 16):
+                ids = lax.broadcasted_iota(jnp.int32, (16, WIDE), 0)
+                along = (ids + (q * 128 + p - P_SIZE // 2)).astype(f32) * SPACING
+                offset = along - where
+                t = offset * offset * gain
+                y = t * bend
+                t = t * (1.0 + y * (1.0 + 2.0 * y))
+                r = t - jnp.round(t)
+                u = r * r
+                sn = r * horner(u, sin_c)
+                cs = horner(u, cos_c)
+                re = re_amp - sn * (re2 * sn + im2 * cs)
+                im = im_amp + sn * (re2 * cs - im2 * sn)
+                parts.append(split(re) + split(im))
+            for c in range(2):
+                lanes = slice(c * P_SIZE + q * 128, c * P_SIZE + (q + 1) * 128)
+                hi = jnp.concatenate([v[2 * c] for v in parts], 0)
+                lo = jnp.concatenate([v[2 * c + 1] for v in parts], 0)
+                d = functools.partial(
+                    lax.dot_general,
+                    dimension_numbers=(((1,), (1,)), ((), ())),
+                    preferred_element_type=f32,
+                )
+                acc[:, lanes] += d(hot, hi) + d(hot, lo)
+
+    out[...] = acc[...]
+
+
+def range_binning(positions, amplitude, cells, bounce, base, span):
+    count = positions.shape[0]
+    sin_c, cos_c = range_trig_coefs(4)
+    whole = pl.BlockSpec(memory_space=pltpu.VMEM)
+    return pl.pallas_call(
+        functools.partial(range_bin_kernel, span=span, sin_c=sin_c, cos_c=cos_c),
+        in_specs=[pl.BlockSpec(memory_space=pltpu.SMEM)] + [whole] * 6,
+        out_specs=whole,
+        out_shape=jax.ShapeDtypeStruct((span, 2 * P_SIZE), f32),
+        scratch_shapes=[
+            pltpu.VMEM((count + SLOTS + WIDE, 128), f32),
+            pltpu.VMEM((span, 2 * P_SIZE), f32),
+        ],
+        name="range_binning",
+    )(
+        base.reshape(1),
+        cells.reshape(count // 128, 128),
+        bounce.reshape(count // 128, 128),
         positions.reshape(1, count),
         amplitude,
         cells.reshape(1, count),
@@ -273,14 +427,13 @@
 
 
 def azimuth_kernel(x, table, out):
-    srcs, bins, lanes = x.shape
-    half = lanes // 2
-    low = lax.broadcasted_iota(jnp.int32, (bins, lanes), 1) < half
+    half = x.shape[0]
+    lanes = 2 * half
+    size = P_SIZE // 4
     quarters = []
     for q in range(4):
-        a, b = x[2 * q], x[2 * q + 1]
-        re = jnp.where(low, a, pltpu.roll(b, half, 1))
-        im = jnp.where(low, pltpu.roll(a, half, 1), b)
+        re = x[:, q * size : (q + 1) * size]
+        im = x[:, P_SIZE + q * size : P_SIZE + (q + 1) * size]
         quarters.append((re, im))
     (r0, i0), (r1, i1), (r2, i2), (r3, i3) = quarters
     sr, si, dr, di = r0 + r2, i0 + i2, r0 - r2, i0 - i2
@@ -291,7 +444,6 @@
         (sr - tr, si - ti),
         (dr - ei, di + er),
     )
-    size = P_SIZE // 4
     low = lax.broadcasted_iota(jnp.int32, (size, lanes), 1) < half
     rows = []
     for k in range(4):
@@ -372,36 +524,48 @@
     theta = theta.reshape(rows * BLOCKS, STOLT)
     cos_p, sin_p = jnp.cos(theta), jnp.sin(theta)
 
-    partial = binning(positions, amplitude, range_cells, bounce, pulse_here * pulses, pulses)
-    partial = partial.reshape(n_scat, bins_scat, 2 * pulses)
-    binned = lax.dynamic_index_in_dim(partial, scat_here, 0, keepdims=False)
-    for shift in range(1, n_scat):
-        other = lax.dynamic_index_in_dim(
-            partial, (scat_here + shift) % n_scat, 0, keepdims=False
-        )
-        ring = [(i, (i + shift) % n_scat) for i in range(n_scat)]
-        binned = binned + lax.ppermute(other, "scat", ring)
-
-    turned = lax.all_to_all(
-        binned.reshape(n_pulse, bins_here, 2 * pulses), "pulse", 0, 0, tiled=True
-    )
     per = STOLT // n_dev
-    packed = 2 * pulses == 128 and 2 * bins_here == 128 and per % 4 == 0 and groups % 8 == 0
+    span = B // n_pulse
+    packed = (
+        span == 128
+        and n_scat == 2
+        and per % 4 == 0
+        and groups % 8 == 0
+        and positions.shape[0] % CHUNK == 0
+    )
     if packed:
         forward, backward = (jnp.asarray(t) for t in quarter_tables())
+        partial = range_binning(
+            positions, amplitude, range_cells, bounce, pulse_here * span, span
+        )
+        own = lax.dynamic_slice_in_dim(partial, scat_here * bins_here, bins_here, 0)
+        other = lax.dynamic_slice_in_dim(partial, (1 - scat_here) * bins_here, bins_here, 0)
+        binned = own + lax.ppermute(other, "scat", [(0, 1), (1, 0)])
         spectrum = pl.pallas_call(
             azimuth_kernel,
             out_shape=jax.ShapeDtypeStruct((n_dev, 4, groups, n), f32),
             name="azimuth",
-        )(turned, forward)
+        )(binned, forward)
         x = lax.all_to_all(spectrum, ("pulse", "scat"), 0, 0, tiled=True)
         x = x.reshape(4 * n_dev, groups, n)
         local = bins_here // BIN_SIDE
         i, s, c, l = np.meshgrid(
             np.arange(n_pulse), np.arange(n_scat), np.arange(2), np.arange(local), indexing="ij"
         )
-        order = (c * BIN_SIDE + s * (BIN_SIDE // n_scat) + i * local + l).reshape(-1)
+        order = (c * BIN_SIDE + (i * n_scat + s) * local + l).reshape(-1)
     else:
+        partial = binning(positions, amplitude, range_cells, bounce, pulse_here * pulses, pulses)
+        partial = partial.reshape(n_scat, bins_scat, 2 * pulses)
+        binned = lax.dynamic_index_in_dim(partial, scat_here, 0, keepdims=False)
+        for shift in range(1, n_scat):
+            other = lax.dynamic_index_in_dim(
+                partial, (scat_here + shift) % n_scat, 0, keepdims=False
+            )
+            ring = [(i, (i + shift) % n_scat) for i in range(n_scat)]
+            binned = binned + lax.ppermute(other, "scat", ring)
+        turned = lax.all_to_all(
+            binned.reshape(n_pulse, bins_here, 2 * pulses), "pulse", 0, 0, tiled=True
+        )
         turned = turned.reshape(n_pulse, bins_here, 2, pulses).transpose(0, 3, 2, 1)
         turned = turned.reshape(P_SIZE, 2 * bins_here)
         k = np.arange(P_SIZE)

time: 102 us -> 90.4 us (0.89)
  waiting for transfers between devices: 11.2 us -> 7.02 us
  starting transfers between devices: 11.4 us -> 7.82 us
  Pallas kernels: 35.7 us -> 33.3 us
    all_to_all x1 -> x0, starting transfers between devices: 7.16 us -> none  [on_device(): lax.all_to_all(binned.reshape(n_pulse, bins_here, 2 * pulses), 'pulse', 0...]
    all_to_all x1 -> x0, waiting for transfers between devices: 4.07 us -> none  [on_device(): lax.all_to_all(binned.reshape(n_pulse, bins_here, 2 * pulses), 'pulse', 0...]
    pallas_call x1, Pallas kernels: 10.2 us -> 7.71 us  [range_binning(): pl.pallas_call(functools.partial(range_bin_kernel, span=span, sin_c=sin_c...]
    all_to_all x1, starting transfers between devices: 3.69 us -> 6.09 us  [on_device(): x = lax.all_to_all(spectrum, ('pulse', 'scat'), 0, 0, tiled=True)]
    ppermute x1, starting transfers between devices: 0.56 us -> 1.73 us  [on_device(): binned = own + lax.ppermute(other, 'scat', [(0, 1), (1, 0)])]
    dynamic_slice x0 -> x1, local copies, waits for them, and re-layouts: none -> 1.04 us  [on_device(): lax.dynamic_slice_in_dim(partial, (1 - scat_here) * bins_here, bins_here, 0)]
  transfers between devices with their start and end apart: 3 -> 2, of which waited for: 3 -> 1; matrix products, arithmetic and copies ran while one was open for 9% -> 11% of each run, Pallas kernels for 0% -> 0%
where the time goes in v1:
time: 90.4 us; the launch traced here: 89.6 us
  Pallas kernels  33.3 us (37%)
  blocking collectives  29 us (32%)
  other arithmetic  8.14 us (9%)
  starting transfers between devices  7.82 us (9%)
  waiting for transfers between devices  7.02 us (8%)
  local copies, waits for them, and re-layouts  4.28 us (5%)
    all_to_all x1, blocking collectives, on_device(): lax.all_to_all(ranged.reshape(n_dev, 2, per, groups, n), ('pulse', 'scat'...  29 us
    pallas_call x1, Pallas kernels, middle(): pl.pallas_call(functools.partial(mid_kernel, subs=subs), grid=(groups //...  19.3 us
    pallas_call x1, Pallas kernels, range_binning(): pl.pallas_call(functools.partial(range_bin_kernel, span=span, sin_c=sin_c...  7.71 us
    all_to_all x1, waiting for transfers between devices, on_device(): x = lax.all_to_all(spectrum, ('pulse', 'scat'), 0, 0, tiled=True)  7.02 us
    all_to_all x1, starting transfers between devices, on_device(): x = lax.all_to_all(spectrum, ('pulse', 'scat'), 0, 0, tiled=True)  6.09 us
    pallas_call x1, Pallas kernels, on_device(): pl.pallas_call(image_kernel, out_shape=jax.ShapeDtypeStruct((2, P_SIZE, w...  3.74 us
    sin x1, other arithmetic, on_device(): cos_p, sin_p = (jnp.cos(theta), jnp.sin(theta))  3.58 us
    pallas_call x1, Pallas kernels, on_device(): pl.pallas_call(azimuth_kernel, out_shape=jax.ShapeDtypeStruct((n_dev, 4,...  2.49 us
  transfers between devices with their start and end apart: 2, of which 1 were waited for; matrix products, arithmetic and copies ran while one was open for 11% of the time, Pallas kernels for 0%

profile of v1, /device:TPU:0, one launch (start us, length us, event | category | flops | bytes accessed | tf_op | source)
XLA Modules:
  0.0 89.6 jit_solution(5107355440285033560)
XLA Ops:
  0.0 7.7 %range_binning.1 = f32[128,1024]{1,0:T(8,128)} custom-call(s32[1]{0:T(128)} %bitcast.base_ref, s32[64,128]{1,0:T(8,128)} %bitcast.31, s32[64,128]{1,0:T(8,128)} %bitcast.33, f32[1,8192]{1,0:T(1,128)} %bitcast.35, f32[2,8192]{1,0:T(2,128)} %amp.1, s32[1,8192]{1,0:T(1,128)} %bitcast.32, s32[1,8192]{1,0:T(1,128)} %bitcast.34), custom_call_target="tpu_custom_call" | custom-call | tf_op jit(solution)/shard_map/range_binning/pallas_call | solution.py:263
  7.7 0.0 copy-start.1
  7.7 1.0 %constant_dynamic-slice_fusion = f32[64,1024]{1,0:T(8,128)S(1)} fusion(f32[128,1024]{1,0:T(8,128)} %range_binning.1, s32[]{:T(128)S(6)} %select_n.21), kind=kLoop, calls=%fused_computation.27 | loop fusion | bytes 524292 | tf_op jit(solution)/shard_map/dynamic_slice | solution.py:542
  8.8 1.7 %collective-permute-start = (f32[64,1024]{1,0:T(8,128)S(1)}, f32[64,1024]{1,0:T(8,128)S(1)}, u32[]{:S(2)}, u32[]{:S(2)}) collective-permute-start(f32[64,1024]{1,0:T(8,128)S(1)} %constant_dynamic-slice_fusion), channel_id=1, source_target_pairs={{0,1},{1,0},{2,3},{3,2},{4,5},{5,4},{6,7},{7,6},{8,9},{9,8},{10,11... | collective-permute-start | bytes 786440 | tf_op jit(solution)/shard_map/ppermute | solution.py:543
  10.5 0.8 broadcast_add_fusion
  11.3 0.8 stack_reshape.4
  12.1 0.1 sub.40
  12.2 0.1 sub.41
  12.2 0.1 div.13
  12.3 0.1 div.14
  12.4 0.1 eq.17
  12.5 1.4 %copy.20.kind = s32[8,256,1]{2,1,0:T(8,128)} copy(s32[8,256,1]{1,0,2:T(8,128)S(1)} %add_bitcast_fusion) | data formatting | bytes 16384 | tf_op jit(solution)/shard_map/reshape | solution.py:518
  13.8 0.0 copy-start
  13.9 3.6 %fusion.4 = (f32[1024,128]{1,0:T(8,128)}, f32[1024,128]{1,0:T(8,128)}) fusion(f32[32,128]{1,0:T(8,128)S(1)} %get-tuple-element.13, f32[1024]{0:T(1024)S(1)} %sub.41, f32[32,128]{1,0:T(8,128)S(1)} %get-tuple-element.14, f32[1024]{0:T(1024)S(1)} %div.14), kind=kLoop, calls=%fused_computation.9 | loop fusion | flops 393216 | bytes 1089536 | tf_op jit(solution)/shard_map/sin | solution.py:525
  17.4 0.0 collective-permute-done
  17.4 0.0 copy-done.1
  17.4 0.7 dynamic-slice_add_fusion.x
  18.2 2.5 %azimuth.1 = f32[16,4,8,128]{3,2,1,0:T(8,128)} custom-call(f32[64,1024]{1,0:T(8,128)} %dynamic-slice_add_fusion.x, bf16[2,4,256,128]{3,2,1,0:T(8,128)(2,1)} %constant.69.clone.table), custom_call_target="tpu_custom_call" | custom-call | tf_op jit(solution)/shard_map/azimuth/pallas_call | solution.py:544
  20.7 6.1 %all-to-all-start = ((f32[16,4,8,128]{3,2,1,0:T(8,128)}), f32[16,4,8,128]{3,2,1,0:T(8,128)S(1)}, u32[]{:S(2)}, u32[]{:S(2)}) async-start(f32[16,4,8,128]{3,2,1,0:T(8,128)} %azimuth.1), calls=%async_computation | async-start | bytes 524288 | tf_op jit(solution)/shard_map/all_to_all | solution.py:549
  26.8 1.1 %fusion.1.hot = bf16[8,256,128]{2,1,0:T(8,128)(2,1)} fusion(s32[8,256]{1,0:T(8,128)S(1)} %eq.17), kind=kLoop, calls=%fused_computation.4 | loop fusion | flops 524288 | bytes 532480 | tf_op jit(solution)/shard_map/convert_element_type | solution.py:517
  27.9 0.0 copy-done
  27.9 1.8 %fusion = (bf16[16,256,128]{2,1,0:T(8,128)(2,1)}, bf16[16,256,128]{2,1,0:T(8,128)(2,1)}) fusion(f32[16,256,128]{2,1,0:T(8,128)S(1)} %copy-done), kind=kLoop, calls=%fused_computation.2 | loop fusion | flops 2097152 | bytes 4194304 | tf_op jit(solution)/shard_map/convert_element_type | solution.py:520
  29.8 7.0 %all-to-all-done = f32[16,4,8,128]{3,2,1,0:T(8,128)S(1)} async-done(((f32[16,4,8,128]{3,2,1,0:T(8,128)}), f32[16,4,8,128]{3,2,1,0:T(8,128)S(1)}, u32[]{:S(2)}, u32[]{:S(2)}) %all-to-all-start) | async-done | bytes 262176 | tf_op jit(solution)/shard_map/all_to_all | solution.py:549
  36.8 0.0 copy-start.2
  36.8 0.7 copy-done.2
  37.5 19.3 %middle.1 = f32[256,8,128]{2,1,0:T(8,128)} custom-call(f32[64,8,128]{2,1,0:T(8,128)} %bitcast.30, f32[1024,128]{1,0:T(8,128)} %get-tuple-element.10.cos_p, f32[1024,128]{1,0:T(8,128)} %get-tuple-element.9.sin_p, bf16[8,256,128]{2,1,0:T(8,128)(2,1)} %fusion.1.hot, s32[8,256,1]{2,1,0:T(8,128)} %copy.20.kind, bf16[16,256,128]{2,1,0:T(8,128)(2,1)} %get-tuple-element.8.bank_hi, ...), custom_call_target="tpu_custom_call" | custom-call | tf_op jit(solution)/shard_map/middle/pallas_call | solution.py:379
  56.8 29.0 %all_to_all.10.x = f32[16,2,8,8,128]{4,3,2,1,0:T(8,128)} all-to-all(f32[16,2,8,8,128]{4,3,2,1,0:T(8,128)} %bitcast.29), channel_id=1, replica_groups=mesh['scene'=2,'pulse'=8,'scat'=2] {'pulse','scat'}, dimensions={0} | all-to-all | bytes 2097152 | tf_op jit(solution)/shard_map/all_to_all | solution.py:588
  85.8 3.7 %image.1 = f32[2,512,256]{2,1,0:T(8,128)} custom-call(f32[16,2,8,8,128]{4,3,2,1,0:T(8,128)} %all_to_all.10.x, bf16[2,4,256,128]{3,2,1,0:T(8,128)(2,1)} %constant.70.clone.table), custom_call_target="tpu_custom_call" | custom-call | tf_op jit(solution)/shard_map/image/pallas_call | solution.py:591
  (6 shorter events, 0.1 us)
Async XLA Ops:
  7.7 9.7 %copy-start.1 = (f32[128,1024]{1,0:T(8,128)S(1)}, f32[128,1024]{1,0:T(8,128)}, u32[]{:S(2)}) copy-start(f32[128,1024]{1,0:T(8,128)} %range_binning.1) | copy-start | bytes 1572868
  8.8 8.7 %collective-permute-start = (f32[64,1024]{1,0:T(8,128)S(1)}, f32[64,1024]{1,0:T(8,128)S(1)}, u32[]{:S(2)}, u32[]{:S(2)}) collective-permute-start(f32[64,1024]{1,0:T(8,128)S(1)} %constant_dynamic-slice_fusion), channel_id=1, source_target_pairs={{0,1},{1,0},{2,3},{3,2},{4,5},{5,4},{6,7},{7,6},{8,9},{9,8},{10,11... | collective-permute-start | bytes 786440 | tf_op jit(solution)/shard_map/ppermute | solution.py:543
  13.8 14.1 %copy-start = (f32[16,256,128]{2,1,0:T(8,128)S(1)}, f32[16,256,128]{2,1,0:T(8,128)}, u32[]{:S(2)}) copy-start(f32[16,256,128]{2,1,0:T(8,128)} %param.21) | copy-start | bytes 6291460
  20.7 16.1 %all-to-all-start = ((f32[16,4,8,128]{3,2,1,0:T(8,128)}), f32[16,4,8,128]{3,2,1,0:T(8,128)S(1)}, u32[]{:S(2)}, u32[]{:S(2)}) async-start(f32[16,4,8,128]{3,2,1,0:T(8,128)} %azimuth.1), calls=%async_computation | async-start | bytes 524288 | tf_op jit(solution)/shard_map/all_to_all | solution.py:549
  36.8 0.7 copy-start.2

commit v2 on v1

--- a/solution.py
+++ b/solution.py
@@ -22,6 +22,7 @@
 SLOTS = 192
 WIDE = 256
 HIGH = lax.Precision.HIGH
+MESH = pl.DeviceIdType.MESH
 f32 = jnp.float32
 bf16 = jnp.bfloat16
 
@@ -426,14 +427,55 @@
     return outs
 
 
-def azimuth_kernel(x, table, out):
-    half = x.shape[0]
+def core_kernel(
+    partial, steps_in, kinds_in, bank, table, ta, wa, tb, tc, wc, td,
+    out,
+    peer, binned, spec, x, xs, cos_p, sin_p, hot, kind, bank_hi, bank_lo, bank_f, os,
+    bank_sem, pair_send, pair_recv, near_send, near_recv, far_send, far_recv,
+    *, n_pulse, n_scat, subs, trig,
+):
+    n_dev = n_pulse * n_scat
+    pulse = lax.axis_index("pulse")
+    scat = lax.axis_index("scat")
+    me = pulse * n_scat + scat
+    half = binned.shape[0]
     lanes = 2 * half
     size = P_SIZE // 4
+    n = GROUP * BLOCKS
+    groups = xs.shape[0]
+    moves = [(a, b) for a in range(n_pulse) for b in range(n_scat) if (a, b) != (0, 0)]
+    moves.sort(key=lambda m: (-min(m[0], n_pulse - m[0]), m))
+
+    def other(a, b):
+        return lax.rem(pulse + a, n_pulse), lax.rem(scat + b, n_scat)
+
+    fetch = pltpu.make_async_copy(bank, bank_f, bank_sem)
+    fetch.start()
+    barrier = pltpu.get_barrier_semaphore()
+    for a, b in moves:
+        p, c = other(a, b)
+        pl.semaphore_signal(
+            barrier, inc=1, device_id={"pulse": p, "scat": c}, device_id_type=MESH
+        )
+    pl.semaphore_wait(barrier, n_dev - 1)
+
+    away = 1 - scat
+    pair = pltpu.make_async_remote_copy(
+        src_ref=partial.at[pl.ds(pl.multiple_of(away * half, half), half), :],
+        dst_ref=peer,
+        send_sem=pair_send,
+        recv_sem=pair_recv,
+        device_id={"pulse": pulse, "scat": away},
+        device_id_type=MESH,
+    )
+    pair.start()
+    pair.wait()
+    binned[...] = partial[pl.ds(pl.multiple_of(scat * half, half), half), :] + peer[...]
+
     quarters = []
     for q in range(4):
-        re = x[:, q * size : (q + 1) * size]
-        im = x[:, P_SIZE + q * size : P_SIZE + (q + 1) * size]
+        re = binned[:, q * size : (q + 1) * size]
+        im = binned[:, P_SIZE + q * size : P_SIZE + (q + 1) * size]
         quarters.append((re, im))
     (r0, i0), (r1, i1), (r2, i2), (r3, i3) = quarters
     sr, si, dr, di = r0 + r2, i0 + i2, r0 - r2, i0 - i2
@@ -452,16 +494,195 @@
         turned = pltpu.roll(g[size:], half, 1)
         rows.append(g[:size] + jnp.where(low, turned, -turned))
     for q, z in enumerate(swap_blocks(rows)):
-        out[:, q] = z.reshape(out.shape[0], out.shape[2], lanes)
+        spec[:, q] = z.reshape(spec.shape[0], groups, n)
+
+    sends = []
+    for i, (a, b) in enumerate(moves):
+        p, c = other(a, b)
+        copy = pltpu.make_async_remote_copy(
+            src_ref=spec.at[p * n_scat + c],
+            dst_ref=x.at[me],
+            send_sem=near_send.at[i],
+            recv_sem=near_recv.at[me],
+            device_id={"pulse": p, "scat": c},
+            device_id_type=MESH,
+        )
+        copy.start()
+        sends.append(copy)
+    x[me] = spec[me]
+
+    block = lax.broadcasted_iota(jnp.int32, (n, STOLT), 0)
+    lane = lax.broadcasted_iota(jnp.int32, (n, STOLT), 1)
+    cols = (lane + (block % BLOCKS) * STOLT).astype(f32)
+    kr = 4.0 * np.pi / 3e8 * (9.6e9 + (cols - F_LEN // 2) * (1.5e8 / F_LEN))
+    flat = []
+    for ref in (steps_in, kinds_in):
+        flat.append(
+            jnp.concatenate([ref[pl.ds(j, groups, stride=GROUP), :] for j in range(GROUP)], 1)
+        )
+    for g in range(groups):
+        row = me * (groups * GROUP) + g * GROUP + block // BLOCKS
+        centered = lax.rem(row + P_SIZE // 2, P_SIZE) - P_SIZE // 2
+        along = 2.0 * np.pi / (P_SIZE * SPACING) * centered.astype(f32)
+        squared = along * along
+        depth = NEAR + B // 2
+        theta = -depth * squared / (jnp.sqrt(kr * kr - squared) + kr)
+        whole = jnp.round(theta * (0.5 / np.pi))
+        for part in turn_parts():
+            theta = theta - whole * part
+        r = theta * (0.5 / np.pi)
+        u = r * r
+        sn = r * horner(u, trig[0])
+        cs = horner(u, trig[1])
+        cos_p[g] = 1.0 - 2.0 * sn * sn
+        sin_p[g] = 2.0 * sn * cs
+        first = jnp.broadcast_to(flat[0][g : g + 1].astype(f32), (n, n)).T
+        first = first + (block // BLOCKS * BLOCKS).astype(f32)
+        spot = lane.astype(f32)
+        hot[g, :n] = jnp.where(first == spot, 1.0, 0.0).astype(bf16)
+        hot[g, n:] = jnp.where(first + 1.0 == spot, 1.0, 0.0).astype(bf16)
+        kind[g] = jnp.broadcast_to(flat[1][g : g + 1].astype(f32), (n, n)).T
+    fetch.wait()
+    for k in range(bank_f.shape[0]):
+        hi, lo = split(bank_f[k])
+        cut = slice(k % 2 * STOLT, (k % 2 + 1) * STOLT)
+        bank_hi[k // 2, :, cut] = hi
+        bank_lo[k // 2, :, cut] = lo
+
+    for i, (a, b) in enumerate(moves):
+        sends[i].wait_send()
+    for a, b in moves:
+        p, c = other(a, b)
+        src = p * n_scat + c
+        pltpu.make_async_copy(x.at[src], x.at[src], near_recv.at[src]).wait()
+    for g in range(groups):
+        xs[g] = x[:, :, g, :].reshape(xs.shape[1], n)
+
+    per = 2 * STOLT // n_dev
+
+    def step(i, carry):
+        parts_hi, parts_lo = [], []
+        for s in range(subs):
+            g = i * subs + s
+            y = dots(split(xs[g]), (ta[0], ta[1]), ((0,), (0,)))
+            yr, yi = y[:, :STOLT], y[:, STOLT:]
+            y = jnp.concatenate([yr * wa[0] - yi * wa[1], yr * wa[1] + yi * wa[0]], 0)
+            z = dots((tb[0], tb[1]), split(y), ((1,), (0,)))
+            zr, zi = z[:n], z[n:]
+            cp, sp = cos_p[g], sin_p[g]
+            z = jnp.concatenate([zr * cp - zi * sp, zr * sp + zi * cp], 1)
+            hi, lo = split(z)
+            picked = jnp.dot(
+                hot[g], jnp.concatenate([hi, lo], 1), preferred_element_type=f32
+            ).astype(bf16)
+            first, second = picked[:n], picked[n:]
+            for c in range(2):
+                for base, keep in ((0, parts_hi), (2 * STOLT, parts_lo)):
+                    cut = slice(base + c * STOLT, base + (c + 1) * STOLT)
+                    keep.append(jnp.concatenate([first[:, cut], second[:, cut]], 1))
+        ghi = jnp.concatenate(parts_hi, 0)
+        glo = jnp.concatenate(parts_lo, 0)
+        kinds = jnp.concatenate([kind[i * subs + s // 2] for s in range(2 * subs)], 0)
+        acc = jnp.zeros((subs * 2 * n, STOLT), f32)
+        for k in range(bank_hi.shape[0]):
+            r = dots((ghi, glo), (bank_hi[k], bank_lo[k]), ((1,), (0,)))
+            for h in range(2):
+                acc = jnp.where(kinds == 2 * k + h, r[:, h * STOLT : (h + 1) * STOLT], acc)
+        for s in range(subs):
+            y = dots(split(acc[s * 2 * n : (s + 1) * 2 * n]), (tc[0], tc[1]), ((0,), (0,)))
+            yr, yi = y[:, :n], y[:, n:]
+            y = jnp.concatenate([yr * wc[0] - yi * wc[1], yr * wc[1] + yi * wc[0]], 0)
+            z = dots((td[0], td[1]), split(y), ((1,), (0,)))
+            os[:, i * subs + s] = z.reshape(n_dev, per, n)
+        span = pl.ds(i * subs, subs)
+        for j, (a, b) in enumerate(moves):
+            p, c = other(a, b)
+            pltpu.make_async_remote_copy(
+                src_ref=os.at[p * n_scat + c, span],
+                dst_ref=out.at[me, span],
+                send_sem=far_send.at[j],
+                recv_sem=far_recv.at[me],
+                device_id={"pulse": p, "scat": c},
+                device_id_type=MESH,
+            ).start()
+        return carry
+
+    lax.fori_loop(0, groups // subs, step, 0)
+    mine = pltpu.make_async_copy(os.at[me], out.at[me], bank_sem)
+    mine.start()
+    mine.wait()
+    for j, (a, b) in enumerate(moves):
+        p, c = other(a, b)
+        src = p * n_scat + c
+        pltpu.make_async_copy(os.at[src], os.at[src], far_send.at[j]).wait()
+        pltpu.make_async_copy(out.at[src], out.at[src], far_recv.at[src]).wait()
+
+
+def turn_parts():
+    parts, rest = [], 2.0 * np.pi
+    for bits in (10, 22, 60):
+        scale = 2.0**bits
+        part = float(np.float32(np.round(rest * scale) / scale))
+        parts.append(part)
+        rest -= part
+    return parts
+
+
+def core(partial, steps_in, kinds_in, bank, table, tables, n_pulse, n_scat):
+    n_dev = n_pulse * n_scat
+    rows = steps_in.shape[0]
+    groups = rows // GROUP
+    subs = 2
+    n = GROUP * BLOCKS
+    span, width = partial.shape
+    half = span // n_scat
+    quads = 2 * half // BIN_SIDE
+    kernels = bank.shape[0]
+    per = 2 * STOLT // n_dev
+    vmem = pl.BlockSpec(memory_space=pltpu.VMEM)
+    dma = pltpu.SemaphoreType.DMA
+    return pl.pallas_call(
+        functools.partial(
+            core_kernel, n_pulse=n_pulse, n_scat=n_scat, subs=subs, trig=range_trig_coefs(5)
+        ),
+        in_specs=[vmem] * 3 + [pl.BlockSpec(memory_space=pl.ANY)] + [vmem] * (1 + len(tables)),
+        out_specs=vmem,
+        out_shape=jax.ShapeDtypeStruct((n_dev, groups, per, n), f32),
+        scratch_shapes=[
+            pltpu.VMEM((half, width), f32),
+            pltpu.VMEM((half, width), f32),
+            pltpu.VMEM((n_dev, quads, groups, n), f32),
+            pltpu.VMEM((n_dev, quads, groups, n), f32),
+            pltpu.VMEM((groups, n_dev * quads, n), f32),
+            pltpu.VMEM((groups, n, STOLT), f32),
+            pltpu.VMEM((groups, n, STOLT), f32),
+            pltpu.VMEM((groups, 2 * n, n), bf16),
+            pltpu.VMEM((groups, n, STOLT), f32),
+            pltpu.VMEM((kernels // 2, 2 * STOLT, 2 * STOLT), bf16),
+            pltpu.VMEM((kernels // 2, 2 * STOLT, 2 * STOLT), bf16),
+            pltpu.VMEM(bank.shape, f32),
+            pltpu.VMEM((n_dev, groups, per, n), f32),
+            dma,
+            dma,
+            dma,
+            dma((n_dev,)),
+            dma((n_dev,)),
+            dma((n_dev,)),
+            dma((n_dev,)),
+        ],
+        compiler_params=pltpu.CompilerParams(collective_id=0, has_side_effects=True),
+        name="core",
+    )(partial, steps_in, kinds_in, bank, table, *tables)
 
 
 def image_kernel(x, table, out):
-    devs, _, per, kh, lanes = x.shape
+    devs, kh, per, lanes = x.shape
+    per = per // 2
     size = P_SIZE // 4
     columns = [[] for _ in range(4)]
     for c in range(2):
         for h in range(per // 4):
-            tiles = [x[:, c, 4 * h + j].reshape(devs * kh, lanes) for j in range(4)]
+            tiles = [x[:, :, c * per + 4 * h + j, :].reshape(devs * kh, lanes) for j in range(4)]
             for k, z in enumerate(swap_blocks(tiles)):
                 columns[k].append(z)
     width = lanes * (per // 4)
@@ -511,6 +732,35 @@
     bins_scat = B // n_scat
     bins_here = bins_scat // n_pulse
 
+    per = STOLT // n_dev
+    span = B // n_pulse
+    packed = (
+        span == 128
+        and n_scat == 2
+        and per % 4 == 0
+        and groups % 8 == 0
+        and positions.shape[0] % CHUNK == 0
+    )
+    if packed:
+        forward, backward = (jnp.asarray(t) for t in quarter_tables())
+        partial = range_binning(
+            positions, amplitude, range_cells, bounce, pulse_here * span, span
+        )
+        local = bins_here // BIN_SIDE
+        i, s, c, l = np.meshgrid(
+            np.arange(n_pulse), np.arange(n_scat), np.arange(2), np.arange(local), indexing="ij"
+        )
+        order = (c * BIN_SIDE + (i * n_scat + s) * local + l).reshape(-1)
+        tables = tuple(jnp.asarray(t) for t in mid_tables(n_dev, order))
+        columns = core(
+            partial, stolt_block, kernel_choice, kernel_bank, forward, tables, n_pulse, n_scat
+        )
+        return pl.pallas_call(
+            image_kernel,
+            out_shape=jax.ShapeDtypeStruct((2, P_SIZE, width), f32),
+            name="image",
+        )(columns, backward)
+
     ids = jnp.arange(GROUP, dtype=jnp.int32)[None, :, None] * BLOCKS
     first = stolt_block.reshape(groups, GROUP, BLOCKS) + ids
     pick = jnp.stack([first, first + 1], 1).reshape(groups, 2 * n, 1)
@@ -524,75 +774,36 @@
     theta = theta.reshape(rows * BLOCKS, STOLT)
     cos_p, sin_p = jnp.cos(theta), jnp.sin(theta)
 
-    per = STOLT // n_dev
-    span = B // n_pulse
-    packed = (
-        span == 128
-        and n_scat == 2
-        and per % 4 == 0
-        and groups % 8 == 0
-        and positions.shape[0] % CHUNK == 0
-    )
-    if packed:
-        forward, backward = (jnp.asarray(t) for t in quarter_tables())
-        partial = range_binning(
-            positions, amplitude, range_cells, bounce, pulse_here * span, span
+    partial = binning(positions, amplitude, range_cells, bounce, pulse_here * pulses, pulses)
+    partial = partial.reshape(n_scat, bins_scat, 2 * pulses)
+    binned = lax.dynamic_index_in_dim(partial, scat_here, 0, keepdims=False)
+    for shift in range(1, n_scat):
+        other = lax.dynamic_index_in_dim(
+            partial, (scat_here + shift) % n_scat, 0, keepdims=False
         )
-        own = lax.dynamic_slice_in_dim(partial, scat_here * bins_here, bins_here, 0)
-        other = lax.dynamic_slice_in_dim(partial, (1 - scat_here) * bins_here, bins_here, 0)
-        binned = own + lax.ppermute(other, "scat", [(0, 1), (1, 0)])
-        spectrum = pl.pallas_call(
-            azimuth_kernel,
-            out_shape=jax.ShapeDtypeStruct((n_dev, 4, groups, n), f32),
-            name="azimuth",
-        )(binned, forward)
-        x = lax.all_to_all(spectrum, ("pulse", "scat"), 0, 0, tiled=True)
-        x = x.reshape(4 * n_dev, groups, n)
-        local = bins_here // BIN_SIDE
-        i, s, c, l = np.meshgrid(
-            np.arange(n_pulse), np.arange(n_scat), np.arange(2), np.arange(local), indexing="ij"
-        )
-        order = (c * BIN_SIDE + (i * n_scat + s) * local + l).reshape(-1)
-    else:
-        partial = binning(positions, amplitude, range_cells, bounce, pulse_here * pulses, pulses)
-        partial = partial.reshape(n_scat, bins_scat, 2 * pulses)
-        binned = lax.dynamic_index_in_dim(partial, scat_here, 0, keepdims=False)
-        for shift in range(1, n_scat):
-            other = lax.dynamic_index_in_dim(
-                partial, (scat_here + shift) % n_scat, 0, keepdims=False
-            )
-            ring = [(i, (i + shift) % n_scat) for i in range(n_scat)]
-            binned = binned + lax.ppermute(other, "scat", ring)
-        turned = lax.all_to_all(
-            binned.reshape(n_pulse, bins_here, 2 * pulses), "pulse", 0, 0, tiled=True
-        )
-        turned = turned.reshape(n_pulse, bins_here, 2, pulses).transpose(0, 3, 2, 1)
-        turned = turned.reshape(P_SIZE, 2 * bins_here)
-        k = np.arange(P_SIZE)
-        angle = 2 * np.pi / P_SIZE * ((k[:, None] * k[None, :]) % P_SIZE)
-        az = jnp.asarray(np.concatenate([np.cos(angle), np.sin(angle)], 0), f32)
-        product = jnp.dot(az, turned, precision=HIGH, preferred_element_type=f32)
-        pc, ps = product[:P_SIZE], product[P_SIZE:]
-        spectrum = pc + jnp.concatenate([ps[:, bins_here:], -ps[:, :bins_here]], 1)
-        az_rows = lax.all_to_all(
-            spectrum.reshape(n_dev, rows, 2 * bins_here), ("pulse", "scat"), 0, 0, tiled=True
-        )
-        x = az_rows.reshape(n_pulse, n_scat, rows, 2, bins_here).transpose(3, 1, 0, 4, 2)
-        x = x.reshape(2, BIN_SIDE, BIN_SIDE, rows).transpose(0, 1, 3, 2)
-        x = x.reshape(2 * BIN_SIDE, groups, n)
-        order = np.arange(2 * BIN_SIDE)
+        ring = [(i, (i + shift) % n_scat) for i in range(n_scat)]
+        binned = binned + lax.ppermute(other, "scat", ring)
+    turned = lax.all_to_all(
+        binned.reshape(n_pulse, bins_here, 2 * pulses), "pulse", 0, 0, tiled=True
+    )
+    turned = turned.reshape(n_pulse, bins_here, 2, pulses).transpose(0, 3, 2, 1)
+    turned = turned.reshape(P_SIZE, 2 * bins_here)
+    k = np.arange(P_SIZE)
+    angle = 2 * np.pi / P_SIZE * ((k[:, None] * k[None, :]) % P_SIZE)
+    az = jnp.asarray(np.concatenate([np.cos(angle), np.sin(angle)], 0), f32)
+    product = jnp.dot(az, turned, precision=HIGH, preferred_element_type=f32)
+    pc, ps = product[:P_SIZE], product[P_SIZE:]
+    spectrum = pc + jnp.concatenate([ps[:, bins_here:], -ps[:, :bins_here]], 1)
+    az_rows = lax.all_to_all(
+        spectrum.reshape(n_dev, rows, 2 * bins_here), ("pulse", "scat"), 0, 0, tiled=True
+    )
+    x = az_rows.reshape(n_pulse, n_scat, rows, 2, bins_here).transpose(3, 1, 0, 4, 2)
+    x = x.reshape(2, BIN_SIDE, BIN_SIDE, rows).transpose(0, 1, 3, 2)
+    x = x.reshape(2 * BIN_SIDE, groups, n)
+    order = np.arange(2 * BIN_SIDE)
 
     tables = tuple(jnp.asarray(t) for t in mid_tables(n_dev, order))
     ranged = middle(x, cos_p, sin_p, hot, kind, bank_hi, bank_lo, tables)
-    if packed:
-        columns = lax.all_to_all(
-            ranged.reshape(n_dev, 2, per, groups, n), ("pulse", "scat"), 0, 0, tiled=True
-        )
-        return pl.pallas_call(
-            image_kernel,
-            out_shape=jax.ShapeDtypeStruct((2, P_SIZE, width), f32),
-            name="image",
-        )(columns, backward)
     columns = lax.all_to_all(
         ranged.reshape(n_dev, 2 * per, rows * BLOCKS), ("pulse", "scat"), 0, 0, tiled=True
     )

time: 90.4 us -> 58 us (0.64)
  blocking collectives: 29 us -> 0 us
  Pallas kernels: 33.3 us -> 57.3 us
  other arithmetic: 8.14 us -> 0 us
  starting transfers between devices: 7.82 us -> 0 us
  waiting for transfers between devices: 7.02 us -> 0 us
  local copies, waits for them, and re-layouts: 4.28 us -> 0 us
    all_to_all x1 -> x0, blocking collectives: 29 us -> none  [on_device(): lax.all_to_all(ranged.reshape(n_dev, 2, per, groups, n), ('pulse', 'scat'...]
    pallas_call x2 -> x1, Pallas kernels: 21.8 us -> 45.6 us  [core(): pl.pallas_call(functools.partial(core_kernel, n_pulse=n_pulse, n_scat=n_s...]
    all_to_all x1 -> x0, waiting for transfers between devices: 7.02 us -> none  [on_device(): x = lax.all_to_all(spectrum, ('pulse', 'scat'), 0, 0, tiled=True)]
    all_to_all x1 -> x0, starting transfers between devices: 6.09 us -> none  [on_device(): x = lax.all_to_all(spectrum, ('pulse', 'scat'), 0, 0, tiled=True)]
    sin x1 -> x0, other arithmetic: 3.58 us -> none  [on_device(): cos_p, sin_p = (jnp.cos(theta), jnp.sin(theta))]
    convert_element_type x2 -> x0, other arithmetic: 2.99 us -> none  [the longest x1 1.84 us: on_device(): bank_lo = (kernel_bank - bank_hi).astype(bf16)]
    ppermute x1 -> x0, starting transfers between devices: 1.73 us -> none  [on_device(): binned = own + lax.ppermute(other, 'scat', [(0, 1), (1, 0)])]
    add x2 -> x0, other arithmetic: 1.53 us -> none  [the longest x1 0.79 us: on_device(): pick = jnp.stack([first, first + 1], 1).reshape(groups, 2 * n, 1)]
  transfers between devices with their start and end apart: 2 -> 0, of which waited for: 1 -> 0; matrix products, arithmetic and copies ran while one was open for 11% -> 0% of each run, Pallas kernels for 0% -> 0%
where the time goes in v2:
time: 58 us; the launch traced here: 57.3 us
  Pallas kernels  57.3 us (99%)
    pallas_call x1, Pallas kernels, core(): pl.pallas_call(functools.partial(core_kernel, n_pulse=n_pulse, n_scat=n_s...  45.6 us
    pallas_call x1, Pallas kernels, range_binning(): pl.pallas_call(functools.partial(range_bin_kernel, span=span, sin_c=sin_c...  7.74 us
    pallas_call x1, Pallas kernels, on_device(): pl.pallas_call(image_kernel, out_shape=jax.ShapeDtypeStruct((2, P_SIZE, w...  3.93 us

profile of v2, /device:TPU:0, one launch (start us, length us, event | category | flops | bytes accessed | tf_op | source)
XLA Modules:
  0.0 57.3 jit_solution(13135355333550046069)
XLA Ops:
  0.0 7.7 %range_binning.1.partial = f32[128,1024]{1,0:T(8,128)} custom-call(s32[1]{0:T(128)} %bitcast.base_ref, s32[64,128]{1,0:T(8,128)} %bitcast.6, s32[64,128]{1,0:T(8,128)} %bitcast.8, f32[1,8192]{1,0:T(1,128)} %bitcast.10, f32[2,8192]{1,0:T(2,128)} %amp.1, s32[1,8192]{1,0:T(1,128)} %bitcast.7, s32[1,8192]{1,0:T(1,128)} %bitcast.9), custom_call_target="tpu_custom_call" | custom-call | tf_op jit(solution)/shard_map/range_binning/pallas_call | solution.py:264
  7.7 45.6 %core.1.x = f32[16,8,16,128]{3,2,1,0:T(8,128)} custom-call(f32[128,1024]{1,0:T(8,128)} %range_binning.1.partial, s32[32,32]{1,0:T(8,128)} %steps_in.1, s32[32,32]{1,0:T(8,128)} %kinds_in.1, f32[16,256,128]{2,1,0:T(8,128)} %bank.1, bf16[2,4,256,128]{3,2,1,0:T(8,128)(2,1)} %constant.22.clone.table, bf16[2,64,256]{2,1,0:T(8,128)(2,1)} %constant.24.clone.ta, ...), custom_call_target="tpu_custom_call" | custom-call | tf_op jit(solution)/shard_map/core/pallas_call | solution.py:644
  53.4 3.9 %image.1 = f32[2,512,256]{2,1,0:T(8,128)} custom-call(f32[16,8,16,128]{3,2,1,0:T(8,128)} %core.1.x, bf16[2,4,256,128]{3,2,1,0:T(8,128)(2,1)} %constant.23.clone.table), custom_call_target="tpu_custom_call" | custom-call | tf_op jit(solution)/shard_map/image/pallas_call | solution.py:758

commit v3 on v2

--- a/solution.py
+++ b/solution.py
@@ -406,7 +406,8 @@
     fwd, inv = [], []
     for low in range(4):
         a = 2 * np.pi / P_SIZE * (((4 * m[:, None] + low) * m[None, :]) % P_SIZE)
-        fwd.append(np.concatenate([np.cos(a), np.sin(a)], 0))
+        turn = a.reshape(-1, 2, q).transpose(1, 0, 2).reshape(q, q)
+        fwd.append(np.concatenate([np.cos(turn), np.sin(turn)], 0))
         inv.append(np.concatenate([np.cos(a.T), np.sin(a.T)], 0) / P_SIZE)
     return np_split(np.stack(fwd)), np_split(np.stack(inv))
 
@@ -430,7 +431,7 @@
 def core_kernel(
     partial, steps_in, kinds_in, bank, table, ta, wa, tb, tc, wc, td,
     out,
-    peer, binned, spec, x, xs, cos_p, sin_p, hot, kind, bank_hi, bank_lo, bank_f, os,
+    peer, binned, spec, x, hot, kind, bank_hi, bank_lo, bank_f, os,
     bank_sem, pair_send, pair_recv, near_send, near_recv, far_send, far_recv,
     *, n_pulse, n_scat, subs, trig,
 ):
@@ -442,7 +443,8 @@
     lanes = 2 * half
     size = P_SIZE // 4
     n = GROUP * BLOCKS
-    groups = xs.shape[0]
+    groups = os.shape[1]
+    pieces = groups // subs
     moves = [(a, b) for a in range(n_pulse) for b in range(n_scat) if (a, b) != (0, 0)]
     moves.sort(key=lambda m: (-min(m[0], n_pulse - m[0]), m))
 
@@ -457,6 +459,21 @@
         pl.semaphore_signal(
             barrier, inc=1, device_id={"pulse": p, "scat": c}, device_id_type=MESH
         )
+
+    block = lax.broadcasted_iota(jnp.int32, (n, STOLT), 0)
+    lane = lax.broadcasted_iota(jnp.int32, (n, STOLT), 1)
+    spot = lane.astype(f32)
+    above = (block // BLOCKS * BLOCKS).astype(f32)
+    flat = []
+    for ref in (steps_in, kinds_in):
+        flat.append(
+            jnp.concatenate([ref[pl.ds(j, groups, stride=GROUP), :] for j in range(GROUP)], 1)
+        )
+    for g in range(groups):
+        first = jnp.broadcast_to(flat[0][g : g + 1].astype(f32), (n, n)).T + above
+        hot[g, :n] = jnp.where(first == spot, 1.0, 0.0).astype(bf16)
+        hot[g, n:] = jnp.where(first + 1.0 == spot, 1.0, 0.0).astype(bf16)
+        kind[g] = jnp.broadcast_to(flat[1][g : g + 1].astype(f32), (n, n)).T
     pl.semaphore_wait(barrier, n_dev - 1)
 
     away = 1 - scat
@@ -469,6 +486,12 @@
         device_id_type=MESH,
     )
     pair.start()
+    fetch.wait()
+    for k in range(bank_f.shape[0]):
+        hi, lo = split(bank_f[k])
+        cut = slice(k % 2 * STOLT, (k % 2 + 1) * STOLT)
+        bank_hi[k // 2, :, cut] = hi
+        bank_lo[k // 2, :, cut] = lo
     pair.wait()
     binned[...] = partial[pl.ds(pl.multiple_of(scat * half, half), half), :] + peer[...]
 
@@ -493,34 +516,36 @@
         g = dots((table[0, k], table[1, k]), split(u), ((1,), (1,)))
         turned = pltpu.roll(g[size:], half, 1)
         rows.append(g[:size] + jnp.where(low, turned, -turned))
+    quads = 2 * half // BIN_SIDE
+    unit = subs * quads
     for q, z in enumerate(swap_blocks(rows)):
-        spec[:, q] = z.reshape(spec.shape[0], groups, n)
-
-    sends = []
-    for i, (a, b) in enumerate(moves):
-        p, c = other(a, b)
-        copy = pltpu.make_async_remote_copy(
-            src_ref=spec.at[p * n_scat + c],
-            dst_ref=x.at[me],
-            send_sem=near_send.at[i],
-            recv_sem=near_recv.at[me],
-            device_id={"pulse": p, "scat": c},
-            device_id_type=MESH,
-        )
-        copy.start()
-        sends.append(copy)
-    x[me] = spec[me]
-
-    block = lax.broadcasted_iota(jnp.int32, (n, STOLT), 0)
-    lane = lax.broadcasted_iota(jnp.int32, (n, STOLT), 1)
+        for h in range(subs):
+            spec[pl.ds(q * subs + h, size // subs, stride=unit), :] = z[
+                h * (size // subs) : (h + 1) * (size // subs)
+            ]
+
+    def piece(dev, i):
+        return pl.ds(pl.multiple_of((dev * pieces + i) * unit, unit), unit)
+
+    own = pl.ds(pl.multiple_of(me * unit, unit), unit)
+    for i in range(pieces):
+        for j, (a, b) in enumerate(moves):
+            p, c = other(a, b)
+            pltpu.make_async_remote_copy(
+                src_ref=spec.at[piece(p * n_scat + c, i), :],
+                dst_ref=x.at[i, own, :],
+                send_sem=near_send.at[j],
+                recv_sem=near_recv.at[i, me],
+                device_id={"pulse": p, "scat": c},
+                device_id_type=MESH,
+            ).start()
+    for i in range(pieces):
+        x[i, own, :] = spec[piece(me, i), :]
+
     cols = (lane + (block % BLOCKS) * STOLT).astype(f32)
     kr = 4.0 * np.pi / 3e8 * (9.6e9 + (cols - F_LEN // 2) * (1.5e8 / F_LEN))
-    flat = []
-    for ref in (steps_in, kinds_in):
-        flat.append(
-            jnp.concatenate([ref[pl.ds(j, groups, stride=GROUP), :] for j in range(GROUP)], 1)
-        )
-    for g in range(groups):
+
+    def phase(g):
         row = me * (groups * GROUP) + g * GROUP + block // BLOCKS
         centered = lax.rem(row + P_SIZE // 2, P_SIZE) - P_SIZE // 2
         along = 2.0 * np.pi / (P_SIZE * SPACING) * centered.astype(f32)
@@ -534,86 +559,73 @@
         u = r * r
         sn = r * horner(u, trig[0])
         cs = horner(u, trig[1])
-        cos_p[g] = 1.0 - 2.0 * sn * sn
-        sin_p[g] = 2.0 * sn * cs
-        first = jnp.broadcast_to(flat[0][g : g + 1].astype(f32), (n, n)).T
-        first = first + (block // BLOCKS * BLOCKS).astype(f32)
-        spot = lane.astype(f32)
-        hot[g, :n] = jnp.where(first == spot, 1.0, 0.0).astype(bf16)
-        hot[g, n:] = jnp.where(first + 1.0 == spot, 1.0, 0.0).astype(bf16)
-        kind[g] = jnp.broadcast_to(flat[1][g : g + 1].astype(f32), (n, n)).T
-    fetch.wait()
-    for k in range(bank_f.shape[0]):
-        hi, lo = split(bank_f[k])
-        cut = slice(k % 2 * STOLT, (k % 2 + 1) * STOLT)
-        bank_hi[k // 2, :, cut] = hi
-        bank_lo[k // 2, :, cut] = lo
-
-    for i, (a, b) in enumerate(moves):
-        sends[i].wait_send()
-    for a, b in moves:
-        p, c = other(a, b)
-        src = p * n_scat + c
-        pltpu.make_async_copy(x.at[src], x.at[src], near_recv.at[src]).wait()
-    for g in range(groups):
-        xs[g] = x[:, :, g, :].reshape(xs.shape[1], n)
+        return 1.0 - 2.0 * sn * sn, 2.0 * sn * cs
 
     per = 2 * STOLT // n_dev
 
-    def step(i, carry):
-        parts_hi, parts_lo = [], []
-        for s in range(subs):
-            g = i * subs + s
-            y = dots(split(xs[g]), (ta[0], ta[1]), ((0,), (0,)))
-            yr, yi = y[:, :STOLT], y[:, STOLT:]
-            y = jnp.concatenate([yr * wa[0] - yi * wa[1], yr * wa[1] + yi * wa[0]], 0)
-            z = dots((tb[0], tb[1]), split(y), ((1,), (0,)))
-            zr, zi = z[:n], z[n:]
-            cp, sp = cos_p[g], sin_p[g]
-            z = jnp.concatenate([zr * cp - zi * sp, zr * sp + zi * cp], 1)
-            hi, lo = split(z)
-            picked = jnp.dot(
-                hot[g], jnp.concatenate([hi, lo], 1), preferred_element_type=f32
-            ).astype(bf16)
-            first, second = picked[:n], picked[n:]
-            for c in range(2):
-                for base, keep in ((0, parts_hi), (2 * STOLT, parts_lo)):
-                    cut = slice(base + c * STOLT, base + (c + 1) * STOLT)
-                    keep.append(jnp.concatenate([first[:, cut], second[:, cut]], 1))
-        ghi = jnp.concatenate(parts_hi, 0)
-        glo = jnp.concatenate(parts_lo, 0)
-        kinds = jnp.concatenate([kind[i * subs + s // 2] for s in range(2 * subs)], 0)
-        acc = jnp.zeros((subs * 2 * n, STOLT), f32)
+    def ranged(i, h):
+        g = i * subs + h
+        cp, sp = phase(g)
+        y = dots(split(x[i, pl.ds(h, n_dev * quads, stride=subs), :]), (ta[0], ta[1]), ((0,), (0,)))
+        yr, yi = y[:, :STOLT], y[:, STOLT:]
+        y = jnp.concatenate([yr * wa[0] - yi * wa[1], yr * wa[1] + yi * wa[0]], 0)
+        z = dots((tb[0], tb[1]), split(y), ((1,), (0,)))
+        zr, zi = z[:n], z[n:]
+        z = jnp.concatenate([zr * cp - zi * sp, zr * sp + zi * cp], 1)
+        hi, lo = split(z)
+        picked = jnp.dot(
+            hot[g], jnp.concatenate([hi, lo], 1), preferred_element_type=f32
+        ).astype(bf16)
+        first, second = picked[:n], picked[n:]
+        parts = [[], []]
+        for c in range(2):
+            for base, keep in zip((0, 2 * STOLT), parts):
+                cut = slice(base + c * STOLT, base + (c + 1) * STOLT)
+                keep.append(jnp.concatenate([first[:, cut], second[:, cut]], 1))
+        ghi, glo = (jnp.concatenate(v, 0) for v in parts)
+        kinds = jnp.concatenate([kind[g]] * 2, 0)
+        acc = jnp.zeros((2 * n, STOLT), f32)
         for k in range(bank_hi.shape[0]):
             r = dots((ghi, glo), (bank_hi[k], bank_lo[k]), ((1,), (0,)))
-            for h in range(2):
-                acc = jnp.where(kinds == 2 * k + h, r[:, h * STOLT : (h + 1) * STOLT], acc)
-        for s in range(subs):
-            y = dots(split(acc[s * 2 * n : (s + 1) * 2 * n]), (tc[0], tc[1]), ((0,), (0,)))
-            yr, yi = y[:, :n], y[:, n:]
-            y = jnp.concatenate([yr * wc[0] - yi * wc[1], yr * wc[1] + yi * wc[0]], 0)
-            z = dots((td[0], td[1]), split(y), ((1,), (0,)))
-            os[:, i * subs + s] = z.reshape(n_dev, per, n)
-        span = pl.ds(i * subs, subs)
+            for v in range(2):
+                acc = jnp.where(kinds == 2 * k + v, r[:, v * STOLT : (v + 1) * STOLT], acc)
+        y = dots(split(acc), (tc[0], tc[1]), ((0,), (0,)))
+        yr, yi = y[:, :n], y[:, n:]
+        y = jnp.concatenate([yr * wc[0] - yi * wc[1], yr * wc[1] + yi * wc[0]], 0)
+        z = dots((td[0], td[1]), split(y), ((1,), (0,)))
+        os[:, g] = z.reshape(n_dev, per, n)
         for j, (a, b) in enumerate(moves):
             p, c = other(a, b)
             pltpu.make_async_remote_copy(
-                src_ref=os.at[p * n_scat + c, span],
-                dst_ref=out.at[me, span],
+                src_ref=os.at[p * n_scat + c, g],
+                dst_ref=out.at[me, g],
                 send_sem=far_send.at[j],
                 recv_sem=far_recv.at[me],
                 device_id={"pulse": p, "scat": c},
                 device_id_type=MESH,
             ).start()
+
+    def step(i, carry):
+        for a, b in moves:
+            p, c = other(a, b)
+            src = p * n_scat + c
+            spot = pl.ds(pl.multiple_of(src * unit, unit), unit)
+            pltpu.make_async_copy(
+                x.at[i, spot, :], x.at[i, spot, :], near_recv.at[i, src]
+            ).wait()
+        for h in range(subs):
+            ranged(i, h)
         return carry
 
-    lax.fori_loop(0, groups // subs, step, 0)
+    lax.fori_loop(0, pieces, step, 0)
     mine = pltpu.make_async_copy(os.at[me], out.at[me], bank_sem)
     mine.start()
     mine.wait()
     for j, (a, b) in enumerate(moves):
         p, c = other(a, b)
         src = p * n_scat + c
+        all_of = spec.at[pl.ds(0, pieces * unit), :]
+        pltpu.make_async_copy(all_of, all_of, near_send.at[j]).wait()
         pltpu.make_async_copy(os.at[src], os.at[src], far_send.at[j]).wait()
         pltpu.make_async_copy(out.at[src], out.at[src], far_recv.at[src]).wait()
 
@@ -651,11 +663,8 @@
         scratch_shapes=[
             pltpu.VMEM((half, width), f32),
             pltpu.VMEM((half, width), f32),
-            pltpu.VMEM((n_dev, quads, groups, n), f32),
-            pltpu.VMEM((n_dev, quads, groups, n), f32),
-            pltpu.VMEM((groups, n_dev * quads, n), f32),
-            pltpu.VMEM((groups, n, STOLT), f32),
-            pltpu.VMEM((groups, n, STOLT), f32),
+            pltpu.VMEM((n_dev * groups * quads, n), f32),
+            pltpu.VMEM((groups // subs, n_dev * subs * quads, n), f32),
             pltpu.VMEM((groups, 2 * n, n), bf16),
             pltpu.VMEM((groups, n, STOLT), f32),
             pltpu.VMEM((kernels // 2, 2 * STOLT, 2 * STOLT), bf16),
@@ -666,7 +675,7 @@
             dma,
             dma,
             dma((n_dev,)),
-            dma((n_dev,)),
+            dma((groups // subs, n_dev)),
             dma((n_dev,)),
             dma((n_dev,)),
         ],

time: 58 us -> 54.5 us (0.940)
  Pallas kernels: 57.3 us -> 54.2 us
    pallas_call x1, Pallas kernels: 45.6 us -> 42.5 us  [core(): pl.pallas_call(functools.partial(core_kernel, n_pulse=n_pulse, n_scat=n_s...]
where the time goes in v3:
time: 54.5 us; the launch traced here: 54.2 us
  Pallas kernels  54.2 us (99%)
    pallas_call x1, Pallas kernels, core(): pl.pallas_call(functools.partial(core_kernel, n_pulse=n_pulse, n_scat=n_s...  42.5 us
    pallas_call x1, Pallas kernels, range_binning(): pl.pallas_call(functools.partial(range_bin_kernel, span=span, sin_c=sin_c...  7.74 us
    pallas_call x1, Pallas kernels, on_device(): pl.pallas_call(image_kernel, out_shape=jax.ShapeDtypeStruct((2, P_SIZE, w...  3.93 us

profile of v3, /device:TPU:0, one launch (start us, length us, event | category | flops | bytes accessed | tf_op | source)
XLA Modules:
  0.0 54.2 jit_solution(12140310664844169677)
XLA Ops:
  0.0 7.7 %range_binning.1.partial = f32[128,1024]{1,0:T(8,128)} custom-call(s32[1]{0:T(128)} %bitcast.base_ref, s32[64,128]{1,0:T(8,128)} %bitcast.6, s32[64,128]{1,0:T(8,128)} %bitcast.8, f32[1,8192]{1,0:T(1,128)} %bitcast.10, f32[2,8192]{1,0:T(2,128)} %amp.1, s32[1,8192]{1,0:T(1,128)} %bitcast.7, s32[1,8192]{1,0:T(1,128)} %bitcast.9), custom_call_target="tpu_custom_call" | custom-call | tf_op jit(solution)/shard_map/range_binning/pallas_call | solution.py:264
  7.7 42.5 %core.1.x = f32[16,8,16,128]{3,2,1,0:T(8,128)} custom-call(f32[128,1024]{1,0:T(8,128)} %range_binning.1.partial, s32[32,32]{1,0:T(8,128)} %steps_in.1, s32[32,32]{1,0:T(8,128)} %kinds_in.1, f32[16,256,128]{2,1,0:T(8,128)} %bank.1, bf16[2,4,256,128]{3,2,1,0:T(8,128)(2,1)} %constant.22.clone.table, bf16[2,64,256]{2,1,0:T(8,128)(2,1)} %constant.24.clone.ta, ...), custom_call_target="tpu_custom_call" | custom-call | tf_op jit(solution)/shard_map/core/pallas_call | solution.py:656
  50.3 3.9 %image.1 = f32[2,512,256]{2,1,0:T(8,128)} custom-call(f32[16,8,16,128]{3,2,1,0:T(8,128)} %core.1.x, bf16[2,4,256,128]{3,2,1,0:T(8,128)(2,1)} %constant.23.clone.table), custom_call_target="tpu_custom_call" | custom-call | tf_op jit(solution)/shard_map/image/pallas_call | solution.py:767
